TPU v7x, 256 devices: a whole 4x4x8 slice. The times are simulated.
256 devices in a mesh: path: 16 (over z, core), tm: 16 (over y, x).
Axes of the slice: x: 4, y: 4, z: 8, core: 2. Of those that a mesh axis runs over, the one named last changes fastest.
Arguments:
- shock_rate: float32 [256, 262144], P('tm', 'path'), may hold values from -6 to 6
- shock_fx: float32 [4, 256, 262144], P(None, 'tm', 'path'), may hold values from -6 to 6
- fx_vol: float32 [4], replicated, may hold values from 0.1 to 0.4
- fx_corr: float32 [4], replicated, may hold values from -0.8 to 0.8
- hazard_scale: float32 [32], replicated, may hold values from 0.03 to 3
- counterparty: int32 [512], replicated, may hold values from 0 to 31
- currency: int32 [512], replicated, may hold values from 0 to 3
- maturity: int32 [512], replicated, may hold values from 1 to 256
- notional: float32 [512], replicated, may hold values from -8 to 8
- strike: float32 [512], replicated, may hold values from 0.7 to 1.3
Outputs:
- profile: float32 [256, 32], P('tm')
- cva: float32 [32], replicated
All inputs are finite; a program needn't handle non-finite values.
Results may differ from a plain program's by a relative error of at most 0.000061.
Values sent between devices are 32-bit elements; how exact they have to be, the bound alone decides.
A program may use at most 64 MiB of HBM per device.

v0:
```python
import math

import jax
import jax.numpy as jnp
from jax import lax
from jax.sharding import Mesh
from jax.sharding import PartitionSpec as P

TM = ("tm_0", "tm_1")


HORIZON = 5.0
RATE_DOM = 0.03
RATE_FOR = 0.01
LOSS_SHARE = 0.6
RATE_SHIFT = 1.5
HIGHEST_PREC = lax.Precision.HIGHEST


def filled_with(shard, identity):
    return jax.tree.map(
        lambda a, e: jnp.broadcast_to(jnp.asarray(e, a.dtype), a.shape), shard, identity
    )


def prefix_by_axis(shard, axes, combine, identity):
    before = start = filled_with(shard, identity)
    so_far = shard
    for axis in reversed(axes):
        devices, mine = (lax.axis_size(axis), lax.axis_index(axis))
        pieces = jax.tree.map(lambda part: lax.all_gather(part, axis), so_far)
        inside, so_far = (start, start)
        for k in range(devices):
            passed = k < mine
            so_far = combine(so_far, jax.tree.map(lambda part: part[k], pieces))
            inside = jax.tree.map(lambda new, old: jnp.where(passed, new, old), so_far, inside)
        before = combine(inside, before)
    return before


def sent_to_all(shard, axis):
    devices = lax.axis_size(axis)
    return lax.all_to_all(
        jnp.broadcast_to(shard[None], (devices, *shard.shape)), axis, 0, 0, tiled=True
    )


def taken_together(shard, axis):
    everything = sent_to_all(shard, axis)
    return jnp.sum(everything, axis=0)


def trade_tables(
    date_rows, counterparty, currency, maturity, notional, strike, cp_count, ccy_count, date_step
):
    is_alive = (date_rows[:, None] < maturity[None, :]).astype(jnp.float32)
    time_left = (maturity[None, :] - date_rows[:, None]).astype(jnp.float32) * date_step
    weight_for = is_alive * notional[None, :] * jnp.exp(-RATE_FOR * time_left)
    weight_dom = is_alive * (notional * strike)[None, :] * jnp.exp(-RATE_DOM * time_left)
    member = (counterparty[None, :] == jnp.arange(cp_count, dtype=jnp.int32)[:, None]).astype(
        jnp.float32
    )
    currency_onehot = (currency[None, :] == jnp.arange(ccy_count, dtype=jnp.int32)[:, None]).astype(
        jnp.float32
    )
    fwd_table = jnp.einsum(
        "ck,tk,jk->tcj", member, weight_for, currency_onehot, precision=HIGHEST_PREC
    )
    dom_table = jnp.einsum("ck,tk->tc", member, weight_dom, precision=HIGHEST_PREC)
    return (fwd_table, dom_table)


def weigh_block(block_item, hazard_scale):
    fwd_table, dom_table, spot, hazard_prev, hazard_cur = block_item
    netted = (
        jnp.einsum("tcj,tjp->tcp", fwd_table, spot, precision=HIGHEST_PREC) - dom_table[:, :, None]
    )
    exposure = jnp.maximum(netted, 0.0)
    scale_row = hazard_scale[None, :, None]
    density = jnp.exp(-scale_row * hazard_prev[:, None, :]) - jnp.exp(
        -scale_row * hazard_cur[:, None, :]
    )
    return jnp.sum(exposure * density, axis=2)


def weigh_dates(fwd_table, dom_table, spot, hazard_prev, hazard_cur, hazard_scale):
    date_count, path_count = hazard_cur.shape
    cp_count = dom_table.shape[1]
    ccy_count = spot.shape[1]
    block_dates = math.gcd(date_count, max(1, 32768 // path_count))
    groups = date_count // block_dates
    blocks = (
        fwd_table.reshape(groups, block_dates, cp_count, ccy_count),
        dom_table.reshape(groups, block_dates, cp_count),
        spot.reshape(groups, block_dates, ccy_count, path_count),
        hazard_prev.reshape(groups, block_dates, path_count),
        hazard_cur.reshape(groups, block_dates, path_count),
    )
    weighed = lax.map(lambda block_item: weigh_block(block_item, hazard_scale), blocks)
    return weighed.reshape(date_count, cp_count)


def local_walk(rate_shock, other_shock, fx_vol, fx_corr, date_step, decay_rate, noise_scale):
    date_count = rate_shock.shape[0]
    date_index = jnp.arange(date_count, dtype=jnp.int32)
    date_gap = date_index[:, None] - date_index[None, :]
    is_below = date_gap >= 0
    powers = jnp.where(is_below, decay_rate ** jnp.maximum(date_gap, 0).astype(jnp.float32), 0.0)
    lower_ones = is_below.astype(jnp.float32)
    rate_walk = noise_scale * jnp.dot(powers, rate_shock, precision=HIGHEST_PREC)
    mix_weight = jnp.sqrt(1.0 - fx_corr * fx_corr)
    mixed = fx_corr[:, None, None] * rate_shock[None] + mix_weight[:, None, None] * other_shock
    moves = (fx_vol * math.sqrt(date_step))[:, None, None] * mixed - (
        0.5 * fx_vol * fx_vol * date_step
    )[:, None, None]
    fx_walk = jnp.einsum("ts,jsp->tjp", lower_ones, moves, precision=HIGHEST_PREC)
    carry_gain = decay_rate ** (jnp.arange(date_count, dtype=jnp.float32) + 1.0)
    return (rate_walk, fx_walk, carry_gain, lower_ones)


def path_intensity(rate_walk, carry_gain, rate_in):
    shifted = rate_walk + carry_gain[:, None] * rate_in[None, :] + RATE_SHIFT
    return 0.1 + 0.5 * shifted * shifted


def finish_paths(intensity, lower_ones, fx_walk, hazard_in, log_in, date_step):
    hazard_cur = hazard_in[None, :] + date_step * jnp.dot(
        lower_ones, intensity, precision=HIGHEST_PREC
    )
    hazard_prev = hazard_cur - date_step * intensity
    spot = jnp.exp(fx_walk + log_in[None])
    return (hazard_prev, hazard_cur, spot)


def combine_affine(earlier, later):
    gain_a, end_a, log_a = earlier
    gain_b, end_b, log_b = later
    return (gain_b * gain_a, gain_b * end_a + end_b, log_a + log_b)


def combine_total(earlier, later):
    return earlier + later


def per_device(
    shock_rate,
    shock_fx,
    fx_vol,
    fx_corr,
    hazard_scale,
    counterparty,
    currency,
    maturity,
    notional,
    strike,
):
    local_dates = shock_rate.shape[0]
    total_dates = local_dates * lax.axis_size(TM)
    total_paths = shock_rate.shape[1] * lax.axis_size("path")
    cp_count = hazard_scale.shape[0]
    ccy_count = fx_vol.shape[0]
    date_step = HORIZON / total_dates
    decay_rate = math.exp(-2.0 / total_dates)
    noise_scale = math.sqrt(1.0 - decay_rate * decay_rate)
    first_date = lax.axis_index(TM) * local_dates
    rate_walk, fx_walk, carry_gain, lower_ones = local_walk(
        shock_rate, shock_fx, fx_vol, fx_corr, date_step, decay_rate, noise_scale
    )
    blank = jnp.zeros_like(rate_walk[0])
    span_gain = jnp.full((1,), decay_rate**local_dates, jnp.float32)
    unit_gain = jnp.ones((1,), jnp.float32)
    log_blank = jnp.zeros_like(fx_walk[0])
    carried = prefix_by_axis(
        (span_gain, rate_walk[-1], fx_walk[-1]), TM, combine_affine, (unit_gain, blank, log_blank)
    )
    rate_in, log_in = (carried[1], carried[2])
    intensity = path_intensity(rate_walk, carry_gain, rate_in)
    block_total = date_step * jnp.sum(intensity, axis=0)
    hazard_in = prefix_by_axis(block_total, TM, combine_total, blank)
    hazard_prev, hazard_cur, spot = finish_paths(
        intensity, lower_ones, fx_walk, hazard_in, log_in, date_step
    )
    date_rows = first_date + jnp.arange(local_dates, dtype=jnp.int32)
    fwd_table, dom_table = trade_tables(
        date_rows,
        counterparty,
        currency,
        maturity,
        notional,
        strike,
        cp_count,
        ccy_count,
        date_step,
    )
    local_sum = weigh_dates(fwd_table, dom_table, spot, hazard_prev, hazard_cur, hazard_scale)
    discount = jnp.exp(-RATE_DOM * date_step * (jnp.arange(total_dates, dtype=jnp.float32) + 1.0))
    profile = taken_together(local_sum, "path") / (total_paths * date_step)
    own_discount = lax.dynamic_slice_in_dim(discount, first_date, local_dates, 0)
    cva = taken_together(
        LOSS_SHARE * date_step * jnp.sum(own_discount[:, None] * profile, axis=0), TM
    )
    return (profile, cva)


def solution(mesh):
    finer = Mesh(mesh.devices.reshape(mesh.shape["path"], 4, 4), ("path", "tm_0", "tm_1"))
    placed = (P(TM, "path"), P(None, TM, "path"), P(), P(), P(), P(), P(), P(), P(), P())
    return jax.shard_map(
        per_device, mesh=finer, in_specs=placed, out_specs=(P(TM, None), P()), check_vma=False
    )
```

profile of v0, /device:TPU:1, one launch (start us, length us, event | category | flops | bytes accessed | tf_op | source)
XLA Modules:
  0.0 230.9 jit_solution(13160290789171733905)
XLA Ops:
  7.9 5.5 %fusion.8 = f32[16,4,16384]{2,0,1:T(8,128)S(1)} fusion(f32[4,16,16384]{2,1,0:T(8,128)} %param.13, f32[4]{0:T(128)S(1)} %get-tuple-element.161, f32[4]{0:T(128)S(1)} %get-tuple-element.166, f32[16,16384]{1,0:T(8,128)} %param.12, f32[4]{0:T(128)} %param.15, f32[4]{0:T(128)S(1)} %get-tuple-element.160), kind=kOutput, calls=%fused_computation.18 | convolution fusion | flops 206569984 | bytes 9437248 | tf_op jit(solution)/shard_map/ts,jsp->tjp/dot_general | solution.py:116
  13.4 1.9 copy-done
  16.6 1.0 convolution_multiply_fusion.1
  17.7 11.0 %all-gather.2 = f32[4,1,16384]{2,1,0:T(1,128)S(1)} all-gather(f32[1,1,16384]{2,1,0:T(1,128)S(1)} %slice_bitcast_fusion.4), channel_id=1, replica_groups=mesh['path'=16,'tm_0'=4,'tm_1'=4] {'tm_1'}, dimensions={0}, use_global_device_ids=true | all-gather | bytes 327680 | tf_op jit(solution)/shard_map/all_gather | solution.py:31
  29.9 8.6 %all-reduce = f32[4]{0:T(128)S(1)} all-reduce(f32[4]{0:T(128)S(1)} %dynamic-update-slice), channel_id=1, replica_groups=mesh['path'=16,'tm_0'=4,'tm_1'=4] {'tm_1'}, use_global_device_ids=true, to_apply=%add | all-reduce | flops 4 | bytes 32
  39.2 1.2 slice_multiply_fusion.2
  41.0 2.1 fusion.84
  43.1 9.4 %all-gather.3 = f32[4,1,16384]{2,1,0:T(1,128)S(1)} all-gather(f32[1,1,16384]{2,1,0:T(1,128)S(1)} %fusion.84), channel_id=1, replica_groups=mesh['path'=16,'tm_0'=4,'tm_1'=4] {'tm_0'}, dimensions={0}, use_global_device_ids=true | all-gather | bytes 327680 | tf_op jit(solution)/shard_map/all_gather | solution.py:31
  53.1 1.4 dynamic-update-slice.1
  54.5 8.5 %all-reduce.1 = f32[4]{0:T(128)S(1)} all-reduce(f32[4]{0:T(128)S(1)} %dynamic-update-slice.1), channel_id=2, replica_groups=mesh['path'=16,'tm_0'=4,'tm_1'=4] {'tm_0'}, use_global_device_ids=true, to_apply=%add.1 | all-reduce | flops 4 | bytes 32
  66.7 4.2 %fusion.27 = f32[1,16384]{1,0:T(1,128)S(1)} fusion(pred[]{:T(512)S(6)} %gt.32, pred[]{:T(512)S(6)} %gt.33, pred[]{:T(512)S(6)} %gt.34, pred[]{:T(512)} %gt.36, pred[]{:T(512)} %gt.37, pred[]{:T(512)} %gt.38, pred[]{:T(512)S(6)} %gt.35, pred[]{:T(512)} %gt.39, f32[4,1,16384]{2,1,0:T(1,128)S(1)} %all-gather.3, f32[]{:T(128)} %bitcast.27, f32[]{:T(128)} %bitcast.28, ...), kind=kLoop, calls=%fused_computation.57 | loop fusion | flops 393216 | bytes 589868 | tf_op jit(solution)/shard_map/add | solution.py:138
  71.4 9.4 %all-gather.1 = f32[65536]{0:T(1024)S(1)} all-gather(f32[16384]{0:T(1024)S(1)} %broadcast_multiply_fusion), channel_id=3, replica_groups=mesh['path'=16,'tm_0'=4,'tm_1'=4] {'tm_1'}, dimensions={0}, use_global_device_ids=true | all-gather | bytes 327680 | tf_op jit(solution)/shard_map/all_gather | solution.py:31
  80.8 9.6 %all-gather.4 = f32[4,1,16384]{2,1,0:T(1,128)S(1)} all-gather(f32[1,1,16384]{2,1,0:T(1,128)S(1)} %bitcast.136), channel_id=1, replica_groups=mesh['path'=16,'tm_0'=4,'tm_1'=4] {'tm_0'}, dimensions={0}, use_global_device_ids=true | all-gather | bytes 327680 | tf_op jit(solution)/shard_map/all_gather | solution.py:31
  90.5 2.0 slice_add_fusion.3
  92.6 2.1 multiply_subtract_fusion
  95.3 1.8 reshape.89
  97.8 34.1 %all-gather.10.cloned.1.call-done = f32[4,4,16384]{2,1,0:T(4,128)} async-done(((f32[1,4,16384]{2,1,0:T(4,128)}), f32[4,4,16384]{2,1,0:T(4,128)}) %all-gather.10.cloned.1.call-update) | async-done | bytes 1048592 | tf_op jit(solution)/shard_map/all_gather | solution.py:31
  132.0 1.4 fusion.22
  133.4 2.8 %add_exponential_fusion = f32[16,4,16384]{2,0,1:T(8,128)S(1)} fusion(f32[16,4,16384]{2,0,1:T(8,128)} %copy-done, f32[4,16384]{1,0:T(4,128)S(1)} %fusion.22), kind=kLoop, calls=%fused_computation.17 | loop fusion | flops 1048576 | bytes 8650752 | tf_op jit(solution)/shard_map/exp | solution.py:131
  136.2 4.6 %copy.24 = f32[16,4,16384]{2,1,0:T(4,128)} copy(f32[16,4,16384]{2,0,1:T(8,128)S(1)} %add_exponential_fusion) | data formatting | bytes 8388608 | tf_op jit(solution)/shard_map/while | solution.py:99
  140.9 50.9 %while.12 = (s32[]{:T(128)}, f32[8,2,32]{2,1,0:T(2,128)S(1)}, f32[8,2,32,4]{2,1,0,3:T(2,128)S(1)}, f32[8,2,4,16384]{3,2,1,0:T(4,128)}, f32[8,2,32]{2,1,0:T(2,128...) while((s32[]{:T(128)}, f32[8,2,32]{2,1,0:T(2,128)S(1)}, ...), condition=%wide.region_3.4_spmd, body=%wide.region_1.3_spmd.sunk | while | flops 57671616 | bytes 1317113 | solution.py:99
  140.9 6.3 %fusion.90 = f32[2,32]{1,0:T(2,128)S(1)} fusion(f32[2,16384]{1,0:T(2,128)S(1)} %get-tuple-element.218, f32[2,16384]{1,0:T(2,128)S(1)} %get-tuple-element.219, f32[32]{0:T(128)S(1)} %bitcast.145, f32[2,32]{1,0:T(2,128)S(1)} %fusion.89, f32[8,2,4,16384]{3,2,1,0:T(4,128)} %get-tuple-element.241, s32[]{:T(128)S(6)} %copy.35, ...), kind=kOutput, calls=%fused_computation.3.clone.1 | convolution fusion | flops 57671616 | bytes 788100 | tf_op jit(solution)/shard_map/while/body/eval_jaxpr/tcj,tjp->tcp/dot_general | solution.py:76
  147.3 6.3 %fusion.90 = f32[2,32]{1,0:T(2,128)S(1)} fusion(f32[2,16384]{1,0:T(2,128)S(1)} %get-tuple-element.218, f32[2,16384]{1,0:T(2,128)S(1)} %get-tuple-element.219, f32[32]{0:T(128)S(1)} %bitcast.145, f32[2,32]{1,0:T(2,128)S(1)} %fusion.89, f32[8,2,4,16384]{3,2,1,0:T(4,128)} %get-tuple-element.241, s32[]{:T(128)S(6)} %copy.35, ...), kind=kOutput, calls=%fused_computation.3.clone.1 | convolution fusion | flops 57671616 | bytes 788100 | tf_op jit(solution)/shard_map/while/body/eval_jaxpr/tcj,tjp->tcp/dot_general | solution.py:76
  153.7 6.3 %fusion.90 = f32[2,32]{1,0:T(2,128)S(1)} fusion(f32[2,16384]{1,0:T(2,128)S(1)} %get-tuple-element.218, f32[2,16384]{1,0:T(2,128)S(1)} %get-tuple-element.219, f32[32]{0:T(128)S(1)} %bitcast.145, f32[2,32]{1,0:T(2,128)S(1)} %fusion.89, f32[8,2,4,16384]{3,2,1,0:T(4,128)} %get-tuple-element.241, s32[]{:T(128)S(6)} %copy.35, ...), kind=kOutput, calls=%fused_computation.3.clone.1 | convolution fusion | flops 57671616 | bytes 788100 | tf_op jit(solution)/shard_map/while/body/eval_jaxpr/tcj,tjp->tcp/dot_general | solution.py:76
  160.0 6.3 %fusion.90 = f32[2,32]{1,0:T(2,128)S(1)} fusion(f32[2,16384]{1,0:T(2,128)S(1)} %get-tuple-element.218, f32[2,16384]{1,0:T(2,128)S(1)} %get-tuple-element.219, f32[32]{0:T(128)S(1)} %bitcast.145, f32[2,32]{1,0:T(2,128)S(1)} %fusion.89, f32[8,2,4,16384]{3,2,1,0:T(4,128)} %get-tuple-element.241, s32[]{:T(128)S(6)} %copy.35, ...), kind=kOutput, calls=%fused_computation.3.clone.1 | convolution fusion | flops 57671616 | bytes 788100 | tf_op jit(solution)/shard_map/while/body/eval_jaxpr/tcj,tjp->tcp/dot_general | solution.py:76
  166.4 6.3 %fusion.90 = f32[2,32]{1,0:T(2,128)S(1)} fusion(f32[2,16384]{1,0:T(2,128)S(1)} %get-tuple-element.218, f32[2,16384]{1,0:T(2,128)S(1)} %get-tuple-element.219, f32[32]{0:T(128)S(1)} %bitcast.145, f32[2,32]{1,0:T(2,128)S(1)} %fusion.89, f32[8,2,4,16384]{3,2,1,0:T(4,128)} %get-tuple-element.241, s32[]{:T(128)S(6)} %copy.35, ...), kind=kOutput, calls=%fused_computation.3.clone.1 | convolution fusion | flops 57671616 | bytes 788100 | tf_op jit(solution)/shard_map/while/body/eval_jaxpr/tcj,tjp->tcp/dot_general | solution.py:76
  172.7 6.3 %fusion.90 = f32[2,32]{1,0:T(2,128)S(1)} fusion(f32[2,16384]{1,0:T(2,128)S(1)} %get-tuple-element.218, f32[2,16384]{1,0:T(2,128)S(1)} %get-tuple-element.219, f32[32]{0:T(128)S(1)} %bitcast.145, f32[2,32]{1,0:T(2,128)S(1)} %fusion.89, f32[8,2,4,16384]{3,2,1,0:T(4,128)} %get-tuple-element.241, s32[]{:T(128)S(6)} %copy.35, ...), kind=kOutput, calls=%fused_computation.3.clone.1 | convolution fusion | flops 57671616 | bytes 788100 | tf_op jit(solution)/shard_map/while/body/eval_jaxpr/tcj,tjp->tcp/dot_general | solution.py:76
  179.1 6.3 %fusion.90 = f32[2,32]{1,0:T(2,128)S(1)} fusion(f32[2,16384]{1,0:T(2,128)S(1)} %get-tuple-element.218, f32[2,16384]{1,0:T(2,128)S(1)} %get-tuple-element.219, f32[32]{0:T(128)S(1)} %bitcast.145, f32[2,32]{1,0:T(2,128)S(1)} %fusion.89, f32[8,2,4,16384]{3,2,1,0:T(4,128)} %get-tuple-element.241, s32[]{:T(128)S(6)} %copy.35, ...), kind=kOutput, calls=%fused_computation.3.clone.1 | convolution fusion | flops 57671616 | bytes 788100 | tf_op jit(solution)/shard_map/while/body/eval_jaxpr/tcj,tjp->tcp/dot_general | solution.py:76
  185.5 6.3 %fusion.90 = f32[2,32]{1,0:T(2,128)S(1)} fusion(f32[2,16384]{1,0:T(2,128)S(1)} %get-tuple-element.218, f32[2,16384]{1,0:T(2,128)S(1)} %get-tuple-element.219, f32[32]{0:T(128)S(1)} %bitcast.145, f32[2,32]{1,0:T(2,128)S(1)} %fusion.89, f32[8,2,4,16384]{3,2,1,0:T(4,128)} %get-tuple-element.241, s32[]{:T(128)S(6)} %copy.35, ...), kind=kOutput, calls=%fused_computation.3.clone.1 | convolution fusion | flops 57671616 | bytes 788100 | tf_op jit(solution)/shard_map/while/body/eval_jaxpr/tcj,tjp->tcp/dot_general | solution.py:76
  192.5 9.8 %all-to-all-start = ((f32[16,1,512]{2,1,0:T(1,128)}), f32[16,1,512]{2,1,0:T(1,128)S(1)}, u32[]{:S(2)}, u32[]{:S(2)}) async-start(f32[16,1,512]{2,1,0:T(1,128)} %reshape.189), calls=%async_computation | async-start | bytes 65536 | tf_op jit(solution)/shard_map/all_to_all | solution.py:43
  202.4 7.3 %all-to-all-done = f32[16,1,512]{2,1,0:T(1,128)S(1)} async-done(((f32[16,1,512]{2,1,0:T(1,128)}), f32[16,1,512]{2,1,0:T(1,128)S(1)}, u32[]{:S(2)}, u32[]{:S(2)}) %all-to-all-start) | async-done | bytes 32800 | tf_op jit(solution)/shard_map/all_to_all | solution.py:43
  211.7 11.8 %all_to_all.11 = f32[16,1,32]{2,1,0:T(1,128)S(1)} all-to-all(f32[16,1,32]{2,1,0:T(1,128)S(1)} %broadcast_in_dim.30), channel_id=1, replica_groups=mesh['path'=16,'tm_0'=4,'tm_1'=4] {'tm_0','tm_1'}, dimensions={0} | all-to-all | bytes 4096 | tf_op jit(solution)/shard_map/all_to_all | solution.py:43
  (95 shorter events, 10.7 us)
Async XLA Ops:
  7.2 83.4 %all-gather.8.cloned.1.call-start = ((), (), s32[]{:S(2)}) async-start(), calls=%async_computation.2 | async-start | bytes 1310720 | tf_op jit(solution)/shard_map/all_gather | solution.py:31
  7.9 8.7 %copy-start.1 = (f32[16,16384]{1,0:T(8,128)S(1)}, f32[16,16384]{1,0:T(8,128)}, u32[]{:S(2)}) copy-start(f32[16,16384]{1,0:T(8,128)} %param.12) | copy-start | bytes 3145732
  7.9 20.8 %copy-start.10 = (u32[256]{0:T(256)S(1)}, u32[256]{0:T(256)}, u32[]{:S(2)}) copy-start(u32[256]{0:T(256)} %constant.103) | copy-start | bytes 3076
  13.4 1.9 copy-start
  15.4 37.1 %copy-start.9 = (u32[256]{0:T(256)S(1)}, u32[256]{0:T(256)}, u32[]{:S(2)}) copy-start(u32[256]{0:T(256)} %constant.108) | copy-start | bytes 3076
  16.5 115.5 %all-gather.10.cloned.1.call-start = ((), (), s32[]{:S(2)}) async-start(), calls=%async_computation.3 | async-start | bytes 1310720 | tf_op jit(solution)/shard_map/all_gather | solution.py:31
  92.5 4.7 %copy-start.3 = (f32[512]{0:T(512)S(1)}, f32[512]{0:T(512)}, u32[]{:S(2)}) copy-start(f32[512]{0:T(512)} %param.20) | copy-start | bytes 6148
  92.5 4.7 %copy-start.4 = (f32[512]{0:T(512)S(1)}, f32[512]{0:T(512)}, u32[]{:S(2)}) copy-start(f32[512]{0:T(512)} %param.21) | copy-start | bytes 6148
  92.5 4.7 %copy-start.8 = (f32[32]{0:T(128)S(1)}, f32[32]{0:T(128)}, u32[]{:S(2)}) copy-start(f32[32]{0:T(128)} %param.16) | copy-start | bytes 388
  92.5 4.7 %copy-start.5 = (s32[512]{0:T(512)S(1)}, s32[512]{0:T(512)}, u32[]{:S(2)}) copy-start(s32[512]{0:T(512)} %param.18) | copy-start | bytes 6148
  92.6 4.8 %copy-start.6 = (s32[512]{0:T(512)S(1)}, s32[512]{0:T(512)}, u32[]{:S(2)}) copy-start(s32[512]{0:T(512)} %param.19) | copy-start | bytes 6148
  92.6 4.8 %copy-start.7 = (s32[512]{0:T(512)S(1)}, s32[512]{0:T(512)}, u32[]{:S(2)}) copy-start(s32[512]{0:T(512)} %param.17) | copy-start | bytes 6148
  92.6 39.4 %copy-start.2 = (f32[4,4,16384]{2,1,0:T(4,128)S(1)}, f32[4,4,16384]{2,1,0:T(4,128)}, u32[]{:S(2)}) copy-start(f32[4,4,16384]{2,1,0:T(4,128)} %all-gather.8.cloned.1.call-done) | copy-start | bytes 3145732
  192.5 17.2 %all-to-all-start = ((f32[16,1,512]{2,1,0:T(1,128)}), f32[16,1,512]{2,1,0:T(1,128)S(1)}, u32[]{:S(2)}, u32[]{:S(2)}) async-start(f32[16,1,512]{2,1,0:T(1,128)} %reshape.189), calls=%async_computation | async-start | bytes 65536 | tf_op jit(solution)/shard_map/all_to_all | solution.py:43
Sparse Core Ops, SparseCore 0:
  16.6 28.3 all-gather.7
  92.7 39.1 all-gather.9
where the time goes:
time: 232 us; the launch traced here: 231 us
  blocking collectives  68.2 us (29%)
  matrix products  59.4 us (26%)
  waiting for transfers between devices  41.5 us (18%)
  between operations  18 us (8%)
  other arithmetic  17.8 us (8%)
  local copies, waits for them, and re-layouts  16 us (7%)
  starting transfers between devices  9.88 us (4%)
    dot_general x8, matrix products, weigh_block(): jnp.einsum('tcj,tjp->tcp', fwd_table, spot, precision=HIGHEST_PREC)  50.3 us
    all_gather x4, blocking collectives, prefix_by_axis(): pieces = jax.tree.map(lambda part: lax.all_gather(part, axis), so_far)  39.3 us
    all_gather x2, waiting for transfers between devices, prefix_by_axis(): pieces = jax.tree.map(lambda part: lax.all_gather(part, axis), so_far)  34.1 us
    unnamed x2, blocking collectives  17.1 us
    all_to_all x1, blocking collectives, sent_to_all(): lax.all_to_all(jnp.broadcast_to(shard[None], (devices, *shard.shape)), ax...  11.8 us
    all_to_all x1, starting transfers between devices, sent_to_all(): lax.all_to_all(jnp.broadcast_to(shard[None], (devices, *shard.shape)), ax...  9.8 us
    all_to_all x1, waiting for transfers between devices, sent_to_all(): lax.all_to_all(jnp.broadcast_to(shard[None], (devices, *shard.shape)), ax...  7.32 us
    add x2, other arithmetic, combine_affine(): return (gain_b * gain_a, gain_b * end_a + end_b, log_a + log_b)  6.25 us
  transfers between devices with their start and end apart: 3, of which 2 were waited for; matrix products, arithmetic and copies ran while one was open for 8% of the time, Pallas kernels for 0%

commit v1 on v0

v1 whole, which is shorter than its diff:
```python
import functools
import math

import jax
import jax.numpy as jnp
from jax import lax
from jax.experimental import pallas as pl
from jax.experimental.pallas import tpu as pltpu
from jax.sharding import PartitionSpec as P

HORIZON = 5.0
RATE_DOM = 0.03
RATE_FOR = 0.01
LOSS_SHARE = 0.6
RATE_SHIFT = 1.5
LOG2E = 1.4426950408889634

CHUNKS = 4
GROUP = 2048
MESH = pl.DeviceIdType.MESH
F32 = jnp.float32
BF16 = jnp.bfloat16


def split3(x):
    high = x.astype(BF16)
    rest = x - high.astype(F32)
    mid = rest.astype(BF16)
    low = (rest - mid.astype(F32)).astype(BF16)
    return high, mid, low


def iota(shape, dim):
    return lax.broadcasted_iota(jnp.int32, shape, dim)


def ones_where(mask):
    return jnp.where(mask, 1.0, 0.0)


def kernel(
    geometry,
    rate_hbm, fx_hbm, vol_s, corr_s, scale_s, cp_ref, ccy_ref, mat_ref, notl_ref, strike_ref,
    prof_out, cva_out,
    xr, xf, log_ref, ab_ref, sum_ref, rcv_ref, pre_ref, st_ref,
    m1_ref, m2_ref, lhs_ref, wf_ref, wd_ref, ns_ref, net_ref, haz_ref, acc_ref,
    part_ref, parts_rcv, cpart_ref, cparts_rcv,
    in_sem, s1_send, s1_recv, s2_send, s2_recv, t_send, t_recv,
):
    n_tm, n_path, paths, dates, cps, ccys, total_dates, total_paths = geometry
    dt = HORIZON / total_dates
    decay = math.exp(-2.0 / total_dates)
    noise = math.sqrt(1.0 - decay * decay)
    width = paths // (CHUNKS * n_tm)
    tiles = CHUNKS * n_tm
    chunk_paths = n_tm * width
    group = min(GROUP, chunk_paths)
    me = lax.axis_index("tm")
    my_path = lax.axis_index("path")

    def load_copies(k):
        lanes = pl.ds(k * chunk_paths, chunk_paths)
        return (
            pltpu.make_async_copy(rate_hbm.at[:, lanes], xr.at[:, lanes], in_sem.at[0, k]),
            pltpu.make_async_copy(fx_hbm.at[:, :, lanes], xf.at[:, :, lanes], in_sem.at[1, k]),
        )

    for k in range(CHUNKS):
        for copy in load_copies(k):
            copy.start()

    barrier = pltpu.get_barrier_semaphore()

    @pl.loop(1, n_tm)
    def _(i):
        pl.semaphore_signal(barrier, inc=1, device_id={"tm": lax.rem(me + i, n_tm)}, device_id_type=MESH)

    @pl.loop(1, n_path)
    def _(i):
        pl.semaphore_signal(
            barrier, inc=1, device_id={"path": lax.rem(my_path + i, n_path)}, device_id_type=MESH
        )

    r, c = iota((96, 256), 0), iota((96, 256), 1)
    s = c - jnp.where(c >= 80, 80, 0) - jnp.where(c >= 160, 80, 0)
    in_ccy, in_date = (s >> 4) - 1, s & 15
    last = jnp.full_like(r, 15)
    out_ccy = jnp.where(r < 64, (r & 31) >> 3, jnp.where((r < 80) | (r == 80), -1, jnp.where(r < 85, r - 81, 9)))
    out_date = jnp.where(r < 64, ((r >> 5) << 3) + (r & 7), jnp.where(r < 80, r - 64, last))
    m1_ref[...] = ones_where((c < 240) & (in_ccy == out_ccy) & (in_date <= out_date)).astype(BF16)
    r, c = iota((48, 128), 0), iota((48, 128), 1)
    s = c & 31
    in_kind, in_date = s >> 4, s & 15
    out_kind = jnp.where(r < 32, r >> 4, jnp.where(r == 37, 0, jnp.where(r == 38, 1, 9)))
    out_date = jnp.where(r < 32, r & 15, jnp.full_like(r, 15))
    m2_ref[...] = ones_where((c < 96) & (in_kind == out_kind) & (in_date <= out_date)).astype(BF16)

    def vec(ref, j):
        return jnp.full((1, 128), ref[j], F32)

    def wide(v, n):
        return jnp.broadcast_to(v[:, :1], (v.shape[0], n))

    c_rate, c_own, c_drift = [], [], []
    for j in range(ccys):
        vol, corr = vec(vol_s, j), vec(corr_s, j)
        c_rate.append(wide(vol * math.sqrt(dt) * corr, group))
        c_own.append(wide(vol * math.sqrt(dt) * jnp.sqrt(1.0 - corr * corr), group))
        c_drift.append(wide(0.5 * vol * vol * dt, group))

    def date_col(n):
        return iota((dates, n), 0).astype(F32)

    log_decay = -2.0 / total_dates

    def walk(first, k, u):
        lanes = pl.ds(pl.multiple_of(first, group), group)
        rate = xr[:, lanes]
        rows = [rate * (noise * jnp.exp(-log_decay * date_col(group)))]
        for j in range(ccys):
            rows.append((c_rate[j] * rate + c_own[j] * xf[j, :, lanes]) - c_drift[j])
        high, mid, low = split3(jnp.concatenate(rows, axis=0))
        right = jnp.concatenate([high, mid, low, jnp.zeros((16, group), BF16)], axis=0)
        out = jnp.dot(m1_ref[...], right, preferred_element_type=F32)
        power = jnp.exp(log_decay * date_col(group))
        shifted = out[64:80] * power + RATE_SHIFT
        cost = dt * (0.1 + 0.5 * shifted * shifted)
        slope = (dt * decay) * power * shifted
        high, mid, low = split3(jnp.concatenate([cost, slope], axis=0))
        right = jnp.concatenate([high, mid, low, jnp.zeros((32, group), BF16)], axis=0)
        out2 = jnp.dot(m2_ref[...], right, preferred_element_type=F32)
        row = iota((8, group), 0)
        ends = jnp.where(row == 0, decay ** (dates - 1), 1.0) * out[80:88] + out2[32:40]
        tile0 = first // width
        for q in range(group // width):
            part = slice(q * width, (q + 1) * width)
            log_ref[tile0 + q] = out[:64, part]
            ab_ref[tile0 + q] = out2[:32, part]
            sum_ref[tile0 + q] = ends[:, part]

    def send1(k, i):
        owner = lax.rem(me + i, n_tm)
        return pltpu.make_async_remote_copy(
            src_ref=sum_ref.at[k * n_tm + owner],
            dst_ref=rcv_ref.at[k, me],
            send_sem=s1_send.at[k],
            recv_sem=s1_recv.at[k],
            device_id={"tm": owner},
            device_id_type=MESH,
        )

    def send2(k, i):
        block = lax.rem(me + i, n_tm)
        return pltpu.make_async_remote_copy(
            src_ref=pre_ref.at[k, block],
            dst_ref=st_ref.at[k * n_tm + me],
            send_sem=s2_send.at[k],
            recv_sem=s2_recv.at[k],
            device_id={"tm": block},
            device_id_type=MESH,
        )

    def all_of(send, recv, k):
        return pltpu.make_async_remote_copy(
            src_ref=rcv_ref.at[k, pl.ds(0, n_tm - 1)],
            dst_ref=rcv_ref.at[k, pl.ds(0, n_tm - 1)],
            send_sem=send.at[k],
            recv_sem=recv.at[k],
            device_id={"tm": me},
            device_id_type=MESH,
        )

    for k in range(CHUNKS):
        for copy in load_copies(k):
            copy.wait()
        for u in range(chunk_paths // group):
            walk(k * chunk_paths + u * group, k, u)
        if k == 0:
            pl.semaphore_wait(barrier, n_tm - 1 + n_path - 1)

        @pl.loop(1, n_tm)
        def _(i):
            send1(k, i).start()

    cp, ccy, mat = cp_ref[...], ccy_ref[...], mat_ref[...]
    trades = cp.shape[1]
    date = iota((dates, trades), 0) + me * dates
    alive = date < mat
    left = (mat - date).astype(F32) * dt
    notl = notl_ref[...]
    wf_ref[...] = jnp.where(alive, notl * jnp.exp(-RATE_FOR * left), 0.0)
    wd_ref[...] = jnp.where(alive, -(notl * strike_ref[...]) * jnp.exp(-RATE_DOM * left), 0.0)
    member = cp == iota((cps, trades), 0)
    col = iota((256, trades), 0)
    pick = jnp.concatenate(
        [
            ones_where((col < 192) & (ccy == ((col & 31) >> 3))).astype(BF16),
            ones_where((col >= 192) & (col < 195)).astype(BF16),
        ],
        axis=1,
    )
    r, c = iota((256, 256), 0), iota((256, 256), 1)
    keep = (c >= 192) | ((r >> 5) == (c & 7))
    part = c >> 5
    is_high = (part == 0) | (part == 3) | (part == 5) | (c == 192)
    is_mid = (part == 1) | (part == 4) | (c == 193)
    for half in range(2):
        blocks = []
        for t in range(half * 8, half * 8 + 8):
            blocks.append(
                jnp.concatenate(
                    [
                        jnp.where(member, wf_ref[t : t + 1], 0.0),
                        jnp.where(member, wd_ref[t : t + 1], 0.0),
                    ],
                    axis=1,
                )
            )
        table = jnp.zeros((256, 256), F32)
        for piece in split3(jnp.concatenate(blocks, axis=0)):
            table = table + lax.dot_general(
                piece, pick, (((1,), (1,)), ((), ())), preferred_element_type=F32
            )
        high, mid, low = split3(jnp.where(keep, table, 0.0))
        chosen = jnp.where(is_high, high.astype(F32), jnp.where(is_mid, mid.astype(F32), low.astype(F32)))
        lhs_ref[half] = chosen.astype(BF16)

    row = iota((cps, 128), 0)
    ns = jnp.zeros((cps, 128), F32)
    for q in range(cps):
        ns = jnp.where(row == q, scale_s[q] * (-LOG2E), ns)
    ns_ref[...] = ns
    acc_ref[...] = jnp.zeros_like(acc_ref)

    block_gain = decay**dates
    block_square = 0.5 * dt * sum(decay ** (2 * (u + 1)) for u in range(dates))
    row = iota((8, width), 0)
    gain = jnp.where(row == 0, block_gain, 1.0)
    for k in range(CHUNKS):
        all_of(s1_send, s1_recv, k).wait_recv()
        rcv_ref[k, me] = sum_ref[k * n_tm + me]
        state = jnp.zeros((8, width), F32)
        for b in range(n_tm):
            pre_ref[k, b] = state
            if b < n_tm - 1:
                x = rcv_ref[k, b]
                rate = jnp.broadcast_to(state[0:1], (8, width))
                slope = jnp.broadcast_to(x[6:7], (8, width))
                extra = rate * (slope + rate * block_square)
                state = gain * state + jnp.where(row < 6, x, 0.0) + jnp.where(row == 5, extra, 0.0)

        @pl.loop(1, n_tm)
        def _(i):
            send2(k, i).start()

        st_ref[k * n_tm + me] = pre_ref[k, me]

    squares = 0.5 * dt * jnp.exp(2 * log_decay) * (1.0 - jnp.exp(2 * log_decay * (date_col(width) + 1.0))) * (
        1.0 / (1.0 - math.exp(2 * log_decay))
    )
    fill = ones_where(iota((64, width), 0) < 16).astype(BF16)

    def prepare(i, slot):
        state = st_ref[i]
        rate, hazard = state[0:1], state[5:6]
        ab = ab_ref[i]
        haz_ref[slot, 0:dates] = hazard + ab[:dates] + rate * (ab[dates:] + rate * squares)
        for half in range(2):
            spots = []
            for j in range(ccys):
                at = half * 32 + j * 8
                spots.append(jnp.exp(log_ref[i, at : at + 8] + state[1 + j : 2 + j]))
            high, mid, low = split3(jnp.concatenate(spots, axis=0))
            right = jnp.concatenate([high, high, high, mid, mid, low, fill], axis=0)
            net_ref[slot, half] = jnp.dot(lhs_ref[half], right, preferred_element_type=F32)

    def weigh(i, slot):
        scale = jnp.concatenate([ns_ref[...]] * (width // 128), axis=1)
        before = jnp.exp2(scale * st_ref[i, 5:6])
        for t in range(dates):
            now = jnp.exp2(scale * haz_ref[slot, t : t + 1])
            at = (t % 8) * cps
            worth = jnp.maximum(net_ref[slot, t // 8, at : at + cps], 0.0) * (before - now)
            before = now
            total = worth[:, :128]
            for q in range(1, width // 128):
                total = total + worth[:, q * 128 : (q + 1) * 128]
            acc_ref[t * cps : (t + 1) * cps] += total

    for k in range(CHUNKS):
        all_of(s2_send, s2_recv, k).wait_recv()

        @pl.loop(0, n_tm)
        def _(o):
            prepare(k * n_tm + o, 0)
            weigh(k * n_tm + o, 0)

    turned = jnp.sum(jnp.transpose(acc_ref[...]), axis=0, keepdims=True)
    part_ref[...] = turned * (1.0 / (total_paths * dt))
    parts_rcv[my_path] = part_ref[...]

    def send_part(i):
        to = lax.rem(my_path + i, n_path)
        return pltpu.make_async_remote_copy(
            src_ref=part_ref,
            dst_ref=parts_rcv.at[my_path],
            send_sem=t_send.at[0],
            recv_sem=t_recv.at[0],
            device_id={"path": to},
            device_id_type=MESH,
        )

    @pl.loop(1, n_path)
    def _(i):
        send_part(i).start()

    def all_parts(ref, n, at, where):
        return pltpu.make_async_remote_copy(
            src_ref=ref.at[pl.ds(0, n - 1)],
            dst_ref=ref.at[pl.ds(0, n - 1)],
            send_sem=t_send.at[at],
            recv_sem=t_recv.at[at],
            device_id=where,
            device_id_type=MESH,
        )

    lane = iota((1, dates * cps), 1)
    at_date = (lane // cps + me * dates).astype(F32)
    discount = (LOSS_SHARE * dt) * jnp.exp(-RATE_DOM * dt * (at_date + 1.0))
    all_parts(parts_rcv, n_path, 0, {"path": my_path}).wait_recv()
    profile = parts_rcv[0]
    for q in range(1, n_path):
        profile = profile + parts_rcv[q]
    prof_out[...] = profile
    terms = profile * discount
    total = terms[:, :128]
    for q in range(1, dates * cps // 128):
        total = total + terms[:, q * 128 : (q + 1) * 128]
    total = total + pltpu.roll(total, 64, 1)
    total = total + pltpu.roll(total, 32, 1)
    cpart_ref[...] = total
    cparts_rcv[me] = total

    def send_cva(i):
        to = lax.rem(me + i, n_tm)
        return pltpu.make_async_remote_copy(
            src_ref=cpart_ref,
            dst_ref=cparts_rcv.at[me],
            send_sem=t_send.at[1],
            recv_sem=t_recv.at[1],
            device_id={"tm": to},
            device_id_type=MESH,
        )

    @pl.loop(1, n_tm)
    def _(i):
        send_cva(i).start()

    for k in range(CHUNKS):
        all_of(s1_send, s1_recv, k).wait_send()
        all_of(s2_send, s2_recv, k).wait_send()
    all_parts(parts_rcv, n_path, 0, {"path": my_path}).wait_send()
    all_parts(cparts_rcv, n_tm, 1, {"tm": me}).wait_recv()
    cva = cparts_rcv[0]
    for q in range(1, n_tm):
        cva = cva + cparts_rcv[q]
    cva_out[...] = cva
    all_parts(cparts_rcv, n_tm, 1, {"tm": me}).wait_send()


def per_device(n_tm, n_path, shock_rate, shock_fx, fx_vol, fx_corr, hazard_scale, *trades):
    dates, paths = shock_rate.shape
    ccys, cps = fx_vol.shape[0], hazard_scale.shape[0]
    geometry = (n_tm, n_path, paths, dates, cps, ccys, dates * n_tm, paths * n_path)
    width = paths // (CHUNKS * n_tm)
    tiles = CHUNKS * n_tm
    count = trades[0].shape[0]
    vmem = functools.partial(pl.BlockSpec, memory_space=pltpu.VMEM)
    smem = functools.partial(pl.BlockSpec, memory_space=pltpu.SMEM)
    anywhere = functools.partial(pl.BlockSpec, memory_space=pl.ANY)
    sems = pltpu.SemaphoreType.DMA
    profile, cva = pl.pallas_call(
        functools.partial(kernel, geometry),
        out_shape=(
            jax.ShapeDtypeStruct((1, dates * cps), F32),
            jax.ShapeDtypeStruct((1, 128), F32),
        ),
        in_specs=[anywhere(), anywhere(), smem(), smem(), smem()] + [vmem()] * 5,
        out_specs=(vmem(), vmem()),
        scratch_shapes=[
            pltpu.VMEM((dates, paths), F32),
            pltpu.VMEM((ccys, dates, paths), F32),
            pltpu.VMEM((tiles, 64, width), F32),
            pltpu.VMEM((tiles, 32, width), F32),
            pltpu.VMEM((tiles, 8, width), F32),
            pltpu.VMEM((CHUNKS, n_tm, 8, width), F32),
            pltpu.VMEM((CHUNKS, n_tm, 8, width), F32),
            pltpu.VMEM((tiles, 8, width), F32),
            pltpu.VMEM((96, 256), BF16),
            pltpu.VMEM((48, 128), BF16),
            pltpu.VMEM((2, 256, 256), BF16),
            pltpu.VMEM((dates, count), F32),
            pltpu.VMEM((dates, count), F32),
            pltpu.VMEM((cps, 128), F32),
            pltpu.VMEM((2, 2, 256, width), F32),
            pltpu.VMEM((2, dates, width), F32),
            pltpu.VMEM((dates * cps, 128), F32),
            pltpu.VMEM((1, dates * cps), F32),
            pltpu.VMEM((n_path, 1, dates * cps), F32),
            pltpu.VMEM((1, 128), F32),
            pltpu.VMEM((n_tm, 1, 128), F32),
            sems((2, CHUNKS)),
            sems((CHUNKS,)),
            sems((CHUNKS,)),
            sems((CHUNKS,)),
            sems((CHUNKS,)),
            sems((2,)),
            sems((2,)),
        ],
        compiler_params=pltpu.CompilerParams(collective_id=0, has_side_effects=True),
    )(shock_rate, shock_fx, fx_vol, fx_corr, hazard_scale, *(a.reshape(1, count) for a in trades))
    return profile.reshape(dates, cps), cva[0, :cps]


def solution(mesh):
    placed = (P("tm", "path"), P(None, "tm", "path"), P(), P(), P(), P(), P(), P(), P(), P())
    return jax.shard_map(
        functools.partial(per_device, mesh.shape["tm"], mesh.shape["path"]),
        mesh=mesh,
        in_specs=placed,
        out_specs=(P("tm", None), P()),
        check_vma=False,
    )
```

time: 232 us -> 53.6 us (0.23)
  blocking collectives: 68.2 us -> 0 us
  matrix products: 59.4 us -> 0 us
  Pallas kernels: 0 us -> 49.1 us
  waiting for transfers between devices: 41.5 us -> 0 us
  between operations: 18 us -> 0.64 us
  other arithmetic: 17.8 us -> 1.34 us
  local copies, waits for them, and re-layouts: 16 us -> 2.29 us
  starting transfers between devices: 9.88 us -> 0 us
    dot_general x13 -> x0, matrix products: 59.4 us -> none  [the longest x8 50.3 us: weigh_block(): jnp.einsum('tcj,tjp->tcp', fwd_table, spot, precision=HIGHEST_PREC)]
    pallas_call x0 -> x1, Pallas kernels: none -> 49.1 us  [per_device(): pl.pallas_call(functools.partial(kernel, geometry), out_shape=(jax.ShapeD...]
    all_gather x4 -> x0, blocking collectives: 39.3 us -> none  [prefix_by_axis(): pieces = jax.tree.map(lambda part: lax.all_gather(part, axis), so_far)]
    all_gather x2 -> x0, waiting for transfers between devices: 34.1 us -> none  [prefix_by_axis(): pieces = jax.tree.map(lambda part: lax.all_gather(part, axis), so_far)]
    unnamed x2 -> x0, blocking collectives: 17.1 us -> none
    all_to_all x1 -> x0, blocking collectives: 11.8 us -> none  [sent_to_all(): lax.all_to_all(jnp.broadcast_to(shard[None], (devices, *shard.shape)), ax...]
    all_to_all x1 -> x0, starting transfers between devices: 9.8 us -> none  [sent_to_all(): lax.all_to_all(jnp.broadcast_to(shard[None], (devices, *shard.shape)), ax...]
    add x5 -> x0, other arithmetic: 7.86 us -> none  [the longest x2 6.25 us: combine_affine(): return (gain_b * gain_a, gain_b * end_a + end_b, log_a + log_b)]
  transfers between devices with their start and end apart: 3 -> 0, of which waited for: 2 -> 0; matrix products, arithmetic and copies ran while one was open for 8% -> 0% of each run, Pallas kernels for 0% -> 0%
where the time goes in v1:
time: 53.6 us; the launch traced here: 53.4 us
  Pallas kernels  49.1 us (92%)
  local copies, waits for them, and re-layouts  2.29 us (4%)
  other arithmetic  1.34 us (2%)
  between operations  0.64 us (1%)
    pallas_call x1, Pallas kernels, per_device(): pl.pallas_call(functools.partial(kernel, geometry), out_shape=(jax.ShapeD...  49.1 us
    pallas_call x1, other arithmetic, per_device(): pl.pallas_call(functools.partial(kernel, geometry), out_shape=(jax.ShapeD...  1.34 us
    squeeze x1, local copies, waits for them, and re-layouts, per_device(): return (profile.reshape(dates, cps), cva[0, :cps])  1.11 us

profile of v1, /device:TPU:1, one launch (start us, length us, event | category | flops | bytes accessed | tf_op | source)
XLA Modules:
  0.0 53.4 jit_solution(12432918858510194589)
XLA Ops:
  0.6 49.1 %shard_map.113 = (f32[1,512]{1,0:T(1,128)}, f32[1,128]{1,0:T(1,128)}) custom-call(f32[16,16384]{1,0:T(8,128)} %rate_hbm.1, f32[4,16,16384]{2,1,0:T(8,128)} %fx_hbm.1, f32[4]{0:T(128)} %vol_s.1, f32[4]{0:T(128)} %corr_s.1, f32[32]{0:T(128)} %scale_s.1, s32[1,512]{1,0:T(1,128)} %bitcast.7, s32[1,512]{1,0:T(1,128)} %bitcast.8, s32[1,512]{1,0:T(1,128)} %bitcast.9, ...), custom_call_target="tpu_custom_call" | custom-call | tf_op jit(solution)/shard_map/pallas_call | solution.py:382
  49.8 0.5 broadcast.3
  50.3 1.3 %reduce.3 = f32[512]{0:T(512)S(1)} reduce(f32[1,512]{1,0:T(1,128)} %get-tuple-element.4, f32[]{:T(128)} %broadcast.3), dimensions={0}, to_apply=%get-tuple-element.4.reduce_sub_computation.3 | reduce | bytes 4100 | tf_op jit(solution)/shard_map/pallas_call | solution.py:382
  51.6 1.1 %slice_bitcast_fusion = f32[32]{0:T(128)} fusion(f32[1,128]{1,0:T(1,128)} %get-tuple-element.5), kind=kLoop, calls=%fused_computation | loop fusion | bytes 256 | tf_op jit(solution)/shard_map/squeeze | solution.py:422
  52.8 0.7 %reshape.27 = f32[16,32]{1,0:T(8,128)} reshape(f32[512]{0:T(512)S(1)} %reduce.3) | data formatting | bytes 4096 | tf_op jit(solution)/shard_map/reshape | solution.py:422

commit v2 on v1

--- a/solution.py
+++ b/solution.py
@@ -34,18 +34,31 @@
     return lax.broadcasted_iota(jnp.int32, shape, dim)
 
 
+def ring_far(i, n):
+    return min(i, n - i)
+
+
+def tm_order(n):
+    return sorted(range(1, n), key=lambda i: -(ring_far(i // 4, n // 4) + ring_far(i % 4, 4)))
+
+
+def path_order(n):
+    return sorted(range(1, n), key=lambda i: -ring_far(i, n))
+
+
 def ones_where(mask):
     return jnp.where(mask, 1.0, 0.0)
 
 
 def kernel(
     geometry,
-    rate_hbm, fx_hbm, vol_s, corr_s, scale_s, cp_ref, ccy_ref, mat_ref, notl_ref, strike_ref,
+    rate_hbm, fx_hbm, vol_hbm, corr_hbm, scale_hbm, cp_hbm, ccy_hbm, mat_hbm, notl_hbm, strike_hbm,
     prof_out, cva_out,
     xr, xf, log_ref, ab_ref, sum_ref, rcv_ref, pre_ref, st_ref,
-    m1_ref, m2_ref, lhs_ref, wf_ref, wd_ref, ns_ref, net_ref, haz_ref, acc_ref,
+    m1_ref, m2_ref, lhs_ref, wf_ref, wd_ref, ns_ref, net0_ref, net1_ref, haz0_ref, haz1_ref, acc_ref,
     part_ref, parts_rcv, cpart_ref, cparts_rcv,
-    in_sem, s1_send, s1_recv, s2_send, s2_recv, t_send, t_recv,
+    vol_s, corr_s, scale_s, cp_ref, ccy_ref, mat_ref, notl_ref, strike_ref,
+    in_sem, small_sem, s1_send, s1_recv, s2_send, s2_recv, t_send, t_recv,
 ):
     n_tm, n_path, paths, dates, cps, ccys, total_dates, total_paths = geometry
     dt = HORIZON / total_dates
@@ -65,18 +78,28 @@
             pltpu.make_async_copy(fx_hbm.at[:, :, lanes], xf.at[:, :, lanes], in_sem.at[1, k]),
         )
 
-    for k in range(CHUNKS):
+    small = [
+        pltpu.make_async_copy(source, target, small_sem.at[q])
+        for q, (source, target) in enumerate(
+            zip(
+                (vol_hbm, corr_hbm, scale_hbm, cp_hbm, ccy_hbm, mat_hbm, notl_hbm, strike_hbm),
+                (vol_s, corr_s, scale_s, cp_ref, ccy_ref, mat_ref, notl_ref, strike_ref),
+            )
+        )
+    ]
+    for copy in load_copies(0):
+        copy.start()
+    for copy in small:
+        copy.start()
+    for k in range(1, CHUNKS):
         for copy in load_copies(k):
             copy.start()
 
     barrier = pltpu.get_barrier_semaphore()
 
-    @pl.loop(1, n_tm)
-    def _(i):
+    for i in tm_order(n_tm):
         pl.semaphore_signal(barrier, inc=1, device_id={"tm": lax.rem(me + i, n_tm)}, device_id_type=MESH)
-
-    @pl.loop(1, n_path)
-    def _(i):
+    for i in path_order(n_path):
         pl.semaphore_signal(
             barrier, inc=1, device_id={"path": lax.rem(my_path + i, n_path)}, device_id_type=MESH
         )
@@ -95,6 +118,9 @@
     out_date = jnp.where(r < 32, r & 15, jnp.full_like(r, 15))
     m2_ref[...] = ones_where((c < 96) & (in_kind == out_kind) & (in_date <= out_date)).astype(BF16)
 
+    small[0].wait()
+    small[1].wait()
+
     def vec(ref, j):
         return jnp.full((1, 128), ref[j], F32)
 
@@ -104,9 +130,9 @@
     c_rate, c_own, c_drift = [], [], []
     for j in range(ccys):
         vol, corr = vec(vol_s, j), vec(corr_s, j)
-        c_rate.append(wide(vol * math.sqrt(dt) * corr, group))
-        c_own.append(wide(vol * math.sqrt(dt) * jnp.sqrt(1.0 - corr * corr), group))
-        c_drift.append(wide(0.5 * vol * vol * dt, group))
+        c_rate.append(wide(vol * (LOG2E * math.sqrt(dt)) * corr, group))
+        c_own.append(wide(vol * (LOG2E * math.sqrt(dt)) * jnp.sqrt(1.0 - corr * corr), group))
+        c_drift.append(wide((0.5 * LOG2E * dt) * vol * vol, group))
 
     def date_col(n):
         return iota((dates, n), 0).astype(F32)
@@ -141,8 +167,8 @@
     def send1(k, i):
         owner = lax.rem(me + i, n_tm)
         return pltpu.make_async_remote_copy(
-            src_ref=sum_ref.at[k * n_tm + owner],
-            dst_ref=rcv_ref.at[k, me],
+            src_ref=sum_ref.at[k * n_tm + owner, pl.ds(0, 7)],
+            dst_ref=rcv_ref.at[k, me, pl.ds(0, 7)],
             send_sem=s1_send.at[k],
             recv_sem=s1_recv.at[k],
             device_id={"tm": owner},
@@ -152,18 +178,18 @@
     def send2(k, i):
         block = lax.rem(me + i, n_tm)
         return pltpu.make_async_remote_copy(
-            src_ref=pre_ref.at[k, block],
-            dst_ref=st_ref.at[k * n_tm + me],
+            src_ref=pre_ref.at[k, block, pl.ds(0, 6)],
+            dst_ref=st_ref.at[k * n_tm + me, pl.ds(0, 6)],
             send_sem=s2_send.at[k],
             recv_sem=s2_recv.at[k],
             device_id={"tm": block},
             device_id_type=MESH,
         )
 
-    def all_of(send, recv, k):
-        return pltpu.make_async_remote_copy(
-            src_ref=rcv_ref.at[k, pl.ds(0, n_tm - 1)],
-            dst_ref=rcv_ref.at[k, pl.ds(0, n_tm - 1)],
+    def all_of(send, recv, k, rows):
+        return pltpu.make_async_remote_copy(
+            src_ref=rcv_ref.at[k, pl.ds(0, n_tm - 1), pl.ds(0, rows)],
+            dst_ref=rcv_ref.at[k, pl.ds(0, n_tm - 1), pl.ds(0, rows)],
             send_sem=send.at[k],
             recv_sem=recv.at[k],
             device_id={"tm": me},
@@ -171,16 +197,21 @@
         )
 
     for k in range(CHUNKS):
-        for copy in load_copies(k):
-            copy.wait()
-        for u in range(chunk_paths // group):
-            walk(k * chunk_paths + u * group, k, u)
+        with jax.named_scope(f"inwait{k}"):
+            for copy in load_copies(k):
+                copy.wait()
+        with jax.named_scope(f"walk{k}"):
+            for u in range(chunk_paths // group):
+                walk(k * chunk_paths + u * group, k, u)
         if k == 0:
-            pl.semaphore_wait(barrier, n_tm - 1 + n_path - 1)
-
-        @pl.loop(1, n_tm)
-        def _(i):
+            with jax.named_scope("barrier"):
+                pl.semaphore_wait(barrier, n_tm - 1 + n_path - 1)
+
+        for i in tm_order(n_tm):
             send1(k, i).start()
+
+    for copy in small[2:]:
+        copy.wait()
 
     cp, ccy, mat = cp_ref[...], ccy_ref[...], mat_ref[...]
     trades = cp.shape[1]
@@ -237,7 +268,8 @@
     row = iota((8, width), 0)
     gain = jnp.where(row == 0, block_gain, 1.0)
     for k in range(CHUNKS):
-        all_of(s1_send, s1_recv, k).wait_recv()
+        with jax.named_scope(f"wait1_{k}"):
+            all_of(s1_send, s1_recv, k, 7).wait_recv()
         rcv_ref[k, me] = sum_ref[k * n_tm + me]
         state = jnp.zeros((8, width), F32)
         for b in range(n_tm):
@@ -249,8 +281,7 @@
                 extra = rate * (slope + rate * block_square)
                 state = gain * state + jnp.where(row < 6, x, 0.0) + jnp.where(row == 5, extra, 0.0)
 
-        @pl.loop(1, n_tm)
-        def _(i):
+        for i in tm_order(n_tm):
             send2(k, i).start()
 
         st_ref[k * n_tm + me] = pre_ref[k, me]
@@ -260,27 +291,29 @@
     )
     fill = ones_where(iota((64, width), 0) < 16).astype(BF16)
 
+    nets, hazs = (net0_ref, net1_ref), (haz0_ref, haz1_ref)
+
     def prepare(i, slot):
         state = st_ref[i]
         rate, hazard = state[0:1], state[5:6]
         ab = ab_ref[i]
-        haz_ref[slot, 0:dates] = hazard + ab[:dates] + rate * (ab[dates:] + rate * squares)
+        hazs[slot][...] = hazard + ab[:dates] + rate * (ab[dates:] + rate * squares)
         for half in range(2):
             spots = []
             for j in range(ccys):
                 at = half * 32 + j * 8
-                spots.append(jnp.exp(log_ref[i, at : at + 8] + state[1 + j : 2 + j]))
+                spots.append(jnp.exp2(log_ref[i, at : at + 8] + state[1 + j : 2 + j]))
             high, mid, low = split3(jnp.concatenate(spots, axis=0))
             right = jnp.concatenate([high, high, high, mid, mid, low, fill], axis=0)
-            net_ref[slot, half] = jnp.dot(lhs_ref[half], right, preferred_element_type=F32)
+            nets[slot][half] = jnp.dot(lhs_ref[half], right, preferred_element_type=F32)
 
     def weigh(i, slot):
         scale = jnp.concatenate([ns_ref[...]] * (width // 128), axis=1)
         before = jnp.exp2(scale * st_ref[i, 5:6])
         for t in range(dates):
-            now = jnp.exp2(scale * haz_ref[slot, t : t + 1])
+            now = jnp.exp2(scale * hazs[slot][t : t + 1])
             at = (t % 8) * cps
-            worth = jnp.maximum(net_ref[slot, t // 8, at : at + cps], 0.0) * (before - now)
+            worth = jnp.maximum(nets[slot][t // 8, at : at + cps], 0.0) * (before - now)
             before = now
             total = worth[:, :128]
             for q in range(1, width // 128):
@@ -288,12 +321,21 @@
             acc_ref[t * cps : (t + 1) * cps] += total
 
     for k in range(CHUNKS):
-        all_of(s2_send, s2_recv, k).wait_recv()
-
-        @pl.loop(0, n_tm)
-        def _(o):
-            prepare(k * n_tm + o, 0)
-            weigh(k * n_tm + o, 0)
+        with jax.named_scope(f"wait2_{k}"):
+            all_of(s2_send, s2_recv, k, 6).wait_recv()
+
+        with jax.named_scope(f"weigh{k}"):
+
+            first = k * n_tm
+            prepare(first, 0)
+
+            @pl.loop(0, n_tm // 2)
+            def _(o):
+                i = first + 2 * o
+                prepare(i + 1, 1)
+                weigh(i, 0)
+                prepare(jnp.minimum(i + 2, first + n_tm - 1), 0)
+                weigh(i + 1, 1)
 
     turned = jnp.sum(jnp.transpose(acc_ref[...]), axis=0, keepdims=True)
     part_ref[...] = turned * (1.0 / (total_paths * dt))
@@ -310,8 +352,7 @@
             device_id_type=MESH,
         )
 
-    @pl.loop(1, n_path)
-    def _(i):
+    for i in path_order(n_path):
         send_part(i).start()
 
     def all_parts(ref, n, at, where):
@@ -327,11 +368,13 @@
     lane = iota((1, dates * cps), 1)
     at_date = (lane // cps + me * dates).astype(F32)
     discount = (LOSS_SHARE * dt) * jnp.exp(-RATE_DOM * dt * (at_date + 1.0))
-    all_parts(parts_rcv, n_path, 0, {"path": my_path}).wait_recv()
+    with jax.named_scope("wait_t1"):
+        all_parts(parts_rcv, n_path, 0, {"path": my_path}).wait_recv()
     profile = parts_rcv[0]
     for q in range(1, n_path):
         profile = profile + parts_rcv[q]
-    prof_out[...] = profile
+    for t in range(dates):
+        prof_out[t : t + 1] = profile[:, t * cps : (t + 1) * cps]
     terms = profile * discount
     total = terms[:, :128]
     for q in range(1, dates * cps // 128):
@@ -352,19 +395,19 @@
             device_id_type=MESH,
         )
 
-    @pl.loop(1, n_tm)
-    def _(i):
+    for i in tm_order(n_tm):
         send_cva(i).start()
 
     for k in range(CHUNKS):
-        all_of(s1_send, s1_recv, k).wait_send()
-        all_of(s2_send, s2_recv, k).wait_send()
+        all_of(s1_send, s1_recv, k, 7).wait_send()
+        all_of(s2_send, s2_recv, k, 6).wait_send()
     all_parts(parts_rcv, n_path, 0, {"path": my_path}).wait_send()
-    all_parts(cparts_rcv, n_tm, 1, {"tm": me}).wait_recv()
+    with jax.named_scope("wait_t2"):
+        all_parts(cparts_rcv, n_tm, 1, {"tm": me}).wait_recv()
     cva = cparts_rcv[0]
     for q in range(1, n_tm):
         cva = cva + cparts_rcv[q]
-    cva_out[...] = cva
+    cva_out[...] = cva[:, :cps]
     all_parts(cparts_rcv, n_tm, 1, {"tm": me}).wait_send()
 
 
@@ -376,16 +419,15 @@
     tiles = CHUNKS * n_tm
     count = trades[0].shape[0]
     vmem = functools.partial(pl.BlockSpec, memory_space=pltpu.VMEM)
-    smem = functools.partial(pl.BlockSpec, memory_space=pltpu.SMEM)
     anywhere = functools.partial(pl.BlockSpec, memory_space=pl.ANY)
     sems = pltpu.SemaphoreType.DMA
     profile, cva = pl.pallas_call(
         functools.partial(kernel, geometry),
         out_shape=(
-            jax.ShapeDtypeStruct((1, dates * cps), F32),
-            jax.ShapeDtypeStruct((1, 128), F32),
+            jax.ShapeDtypeStruct((dates, cps), F32),
+            jax.ShapeDtypeStruct((1, cps), F32),
         ),
-        in_specs=[anywhere(), anywhere(), smem(), smem(), smem()] + [vmem()] * 5,
+        in_specs=[anywhere()] * 10,
         out_specs=(vmem(), vmem()),
         scratch_shapes=[
             pltpu.VMEM((dates, paths), F32),
@@ -402,14 +444,25 @@
             pltpu.VMEM((dates, count), F32),
             pltpu.VMEM((dates, count), F32),
             pltpu.VMEM((cps, 128), F32),
-            pltpu.VMEM((2, 2, 256, width), F32),
-            pltpu.VMEM((2, dates, width), F32),
+            pltpu.VMEM((2, 256, width), F32),
+            pltpu.VMEM((2, 256, width), F32),
+            pltpu.VMEM((dates, width), F32),
+            pltpu.VMEM((dates, width), F32),
             pltpu.VMEM((dates * cps, 128), F32),
             pltpu.VMEM((1, dates * cps), F32),
             pltpu.VMEM((n_path, 1, dates * cps), F32),
             pltpu.VMEM((1, 128), F32),
             pltpu.VMEM((n_tm, 1, 128), F32),
+            pltpu.SMEM((ccys,), F32),
+            pltpu.SMEM((ccys,), F32),
+            pltpu.SMEM((cps,), F32),
+            pltpu.VMEM((1, count), jnp.int32),
+            pltpu.VMEM((1, count), jnp.int32),
+            pltpu.VMEM((1, count), jnp.int32),
+            pltpu.VMEM((1, count), F32),
+            pltpu.VMEM((1, count), F32),
             sems((2, CHUNKS)),
+            sems((8,)),
             sems((CHUNKS,)),
             sems((CHUNKS,)),
             sems((CHUNKS,)),
@@ -419,7 +472,7 @@
         ],
         compiler_params=pltpu.CompilerParams(collective_id=0, has_side_effects=True),
     )(shock_rate, shock_fx, fx_vol, fx_corr, hazard_scale, *(a.reshape(1, count) for a in trades))
-    return profile.reshape(dates, cps), cva[0, :cps]
+    return profile, cva.reshape(cps)
 
 
 def solution(mesh):

time: 53.6 us -> 46.8 us (0.87)
  Pallas kernels: 49.1 us -> 43.5 us
  other arithmetic: 1.34 us -> 0 us
    pallas_call x1, Pallas kernels: 49.1 us -> 43.5 us  [per_device(): pl.pallas_call(functools.partial(kernel, geometry), out_shape=(jax.ShapeD...]
    unnamed x0 -> x2, local copies, waits for them, and re-layouts: none -> 2.43 us
    pallas_call x1 -> x0, other arithmetic: 1.34 us -> none  [per_device(): pl.pallas_call(functools.partial(kernel, geometry), out_shape=(jax.ShapeD...]
    squeeze x1 -> x0, local copies, waits for them, and re-layouts: 1.11 us -> none  [per_device(): return (profile.reshape(dates, cps), cva[0, :cps])]
    reshape x1 -> x0, local copies, waits for them, and re-layouts: 0.67 us -> none  [per_device(): return (profile.reshape(dates, cps), cva[0, :cps])]
where the time goes in v2:
time: 46.8 us; the launch traced here: 46.6 us
  Pallas kernels  43.5 us (93%)
  local copies, waits for them, and re-layouts  2.43 us (5%)
  between operations  0.64 us (1%)
    pallas_call x1, Pallas kernels, per_device(): pl.pallas_call(functools.partial(kernel, geometry), out_shape=(jax.ShapeD...  43.5 us
    unnamed x2, local copies, waits for them, and re-layouts  2.43 us

profile of v2, /device:TPU:1, one launch (start us, length us, event | category | flops | bytes accessed | tf_op | source)
XLA Modules:
  0.0 46.6 jit_solution(3936906666122633827)
XLA Ops:
  0.6 43.5 %shard_map.113 = (f32[16,32]{1,0:T(8,128)}, f32[1,32]{1,0:T(1,128)}) custom-call(f32[16,16384]{1,0:T(8,128)} %rate_hbm.1, f32[4,16,16384]{2,1,0:T(8,128)} %fx_hbm.1, f32[4]{0:T(128)} %vol_hbm.1, f32[4]{0:T(128)} %corr_hbm.1, f32[32]{0:T(128)} %scale_hbm.1, s32[1,512]{1,0:T(1,128)} %bitcast.6, s32[1,512]{1,0:T(1,128)} %bitcast.7, s32[1,512]{1,0:T(1,128)} %bitcast.8, ...), custom_call_target="tpu_custom_call" | custom-call | tf_op jit(solution)/shard_map/pallas_call | solution.py:424
  44.2 1.3 %copy.14 = f32[16,32]{1,0:T(8,128)} copy(f32[16,32]{1,0:T(8,128)} %get-tuple-element.8) | data formatting | bytes 4096
  45.5 1.1 %copy.15 = f32[32]{0:T(128)} copy(f32[32]{0:T(128)} %bitcast.11) | data formatting | bytes 256

commit v3 on v2

--- a/solution.py
+++ b/solution.py
@@ -15,8 +15,9 @@
 RATE_SHIFT = 1.5
 LOG2E = 1.4426950408889634
 
-CHUNKS = 4
-GROUP = 2048
+CHUNKS = 8
+TILE = 256
+AHEAD = 4
 MESH = pl.DeviceIdType.MESH
 F32 = jnp.float32
 BF16 = jnp.bfloat16
@@ -55,7 +56,7 @@
     rate_hbm, fx_hbm, vol_hbm, corr_hbm, scale_hbm, cp_hbm, ccy_hbm, mat_hbm, notl_hbm, strike_hbm,
     prof_out, cva_out,
     xr, xf, log_ref, ab_ref, sum_ref, rcv_ref, pre_ref, st_ref,
-    m1_ref, m2_ref, lhs_ref, wf_ref, wd_ref, ns_ref, net0_ref, net1_ref, haz0_ref, haz1_ref, acc_ref,
+    m1_ref, m2_ref, lhs_ref, wf_ref, wd_ref, ns_ref, net0_ref, net1_ref, net2_ref, net3_ref, haz0_ref, haz1_ref, haz2_ref, haz3_ref, acc_ref,
     part_ref, parts_rcv, cpart_ref, cparts_rcv,
     vol_s, corr_s, scale_s, cp_ref, ccy_ref, mat_ref, notl_ref, strike_ref,
     in_sem, small_sem, s1_send, s1_recv, s2_send, s2_recv, t_send, t_recv,
@@ -64,10 +65,11 @@
     dt = HORIZON / total_dates
     decay = math.exp(-2.0 / total_dates)
     noise = math.sqrt(1.0 - decay * decay)
-    width = paths // (CHUNKS * n_tm)
-    tiles = CHUNKS * n_tm
-    chunk_paths = n_tm * width
-    group = min(GROUP, chunk_paths)
+    piece = paths // (CHUNKS * n_tm)
+    width = TILE
+    tiles = paths // width
+    per_tile = width // piece
+    group = chunk_paths = n_tm * piece
     me = lax.axis_index("tm")
     my_path = lax.axis_index("path")
 
@@ -139,7 +141,7 @@
 
     log_decay = -2.0 / total_dates
 
-    def walk(first, k, u):
+    def walk(first):
         lanes = pl.ds(pl.multiple_of(first, group), group)
         rate = xr[:, lanes]
         rows = [rate * (noise * jnp.exp(-log_decay * date_col(group)))]
@@ -157,12 +159,12 @@
         out2 = jnp.dot(m2_ref[...], right, preferred_element_type=F32)
         row = iota((8, group), 0)
         ends = jnp.where(row == 0, decay ** (dates - 1), 1.0) * out[80:88] + out2[32:40]
-        tile0 = first // width
         for q in range(group // width):
             part = slice(q * width, (q + 1) * width)
-            log_ref[tile0 + q] = out[:64, part]
-            ab_ref[tile0 + q] = out2[:32, part]
-            sum_ref[tile0 + q] = ends[:, part]
+            log_ref[first // width + q] = out[:64, part]
+            ab_ref[first // width + q] = out2[:32, part]
+        for q in range(n_tm):
+            sum_ref[first // piece + q] = ends[:, q * piece : (q + 1) * piece]
 
     def send1(k, i):
         owner = lax.rem(me + i, n_tm)
@@ -196,19 +198,46 @@
             device_id_type=MESH,
         )
 
-    for k in range(CHUNKS):
+    def walk_and_send(k):
         with jax.named_scope(f"inwait{k}"):
             for copy in load_copies(k):
                 copy.wait()
         with jax.named_scope(f"walk{k}"):
-            for u in range(chunk_paths // group):
-                walk(k * chunk_paths + u * group, k, u)
+            walk(k * chunk_paths)
         if k == 0:
             with jax.named_scope("barrier"):
                 pl.semaphore_wait(barrier, n_tm - 1 + n_path - 1)
-
         for i in tm_order(n_tm):
             send1(k, i).start()
+
+    block_gain = decay**dates
+    block_square = 0.5 * dt * sum(decay ** (2 * (u + 1)) for u in range(dates))
+    kind = iota((8, piece), 0)
+    gain = jnp.where(kind == 0, block_gain, 1.0)
+
+    def own(k):
+        with jax.named_scope("wait1"):
+            all_of(s1_send, s1_recv, k, 7).wait_recv()
+        rcv_ref[k, me] = sum_ref[k * n_tm + me]
+        state = jnp.zeros((8, piece), F32)
+        for b in range(n_tm):
+            pre_ref[k, b] = state
+            if b < n_tm - 1:
+                x = rcv_ref[k, b]
+                rate = jnp.broadcast_to(state[0:1], (8, piece))
+                slope = jnp.broadcast_to(x[6:7], (8, piece))
+                extra = rate * (slope + rate * block_square)
+                state = gain * state + jnp.where(kind < 6, x, 0.0) + jnp.where(kind == 5, extra, 0.0)
+        for i in tm_order(n_tm):
+            send2(k, i).start()
+        st_ref[k * n_tm + me] = pre_ref[k, me]
+
+    for k in range(6):
+        walk_and_send(k)
+    own(0)
+    walk_and_send(6)
+    own(1)
+    walk_and_send(7)
 
     for copy in small[2:]:
         copy.wait()
@@ -248,9 +277,9 @@
                 )
             )
         table = jnp.zeros((256, 256), F32)
-        for piece in split3(jnp.concatenate(blocks, axis=0)):
+        for term in split3(jnp.concatenate(blocks, axis=0)):
             table = table + lax.dot_general(
-                piece, pick, (((1,), (1,)), ((), ())), preferred_element_type=F32
+                term, pick, (((1,), (1,)), ((), ())), preferred_element_type=F32
             )
         high, mid, low = split3(jnp.where(keep, table, 0.0))
         chosen = jnp.where(is_high, high.astype(F32), jnp.where(is_mid, mid.astype(F32), low.astype(F32)))
@@ -263,38 +292,18 @@
     ns_ref[...] = ns
     acc_ref[...] = jnp.zeros_like(acc_ref)
 
-    block_gain = decay**dates
-    block_square = 0.5 * dt * sum(decay ** (2 * (u + 1)) for u in range(dates))
-    row = iota((8, width), 0)
-    gain = jnp.where(row == 0, block_gain, 1.0)
-    for k in range(CHUNKS):
-        with jax.named_scope(f"wait1_{k}"):
-            all_of(s1_send, s1_recv, k, 7).wait_recv()
-        rcv_ref[k, me] = sum_ref[k * n_tm + me]
-        state = jnp.zeros((8, width), F32)
-        for b in range(n_tm):
-            pre_ref[k, b] = state
-            if b < n_tm - 1:
-                x = rcv_ref[k, b]
-                rate = jnp.broadcast_to(state[0:1], (8, width))
-                slope = jnp.broadcast_to(x[6:7], (8, width))
-                extra = rate * (slope + rate * block_square)
-                state = gain * state + jnp.where(row < 6, x, 0.0) + jnp.where(row == 5, extra, 0.0)
-
-        for i in tm_order(n_tm):
-            send2(k, i).start()
-
-        st_ref[k * n_tm + me] = pre_ref[k, me]
+    own(2)
+    own(3)
 
     squares = 0.5 * dt * jnp.exp(2 * log_decay) * (1.0 - jnp.exp(2 * log_decay * (date_col(width) + 1.0))) * (
         1.0 / (1.0 - math.exp(2 * log_decay))
     )
     fill = ones_where(iota((64, width), 0) < 16).astype(BF16)
 
-    nets, hazs = (net0_ref, net1_ref), (haz0_ref, haz1_ref)
+    nets, hazs = (net0_ref, net1_ref, net2_ref, net3_ref), (haz0_ref, haz1_ref, haz2_ref, haz3_ref)
 
     def prepare(i, slot):
-        state = st_ref[i]
+        state = jnp.concatenate([st_ref[i * per_tile + q] for q in range(per_tile)], axis=1)
         rate, hazard = state[0:1], state[5:6]
         ab = ab_ref[i]
         hazs[slot][...] = hazard + ab[:dates] + rate * (ab[dates:] + rate * squares)
@@ -307,35 +316,59 @@
             right = jnp.concatenate([high, high, high, mid, mid, low, fill], axis=0)
             nets[slot][half] = jnp.dot(lhs_ref[half], right, preferred_element_type=F32)
 
-    def weigh(i, slot):
-        scale = jnp.concatenate([ns_ref[...]] * (width // 128), axis=1)
-        before = jnp.exp2(scale * st_ref[i, 5:6])
-        for t in range(dates):
-            now = jnp.exp2(scale * hazs[slot][t : t + 1])
-            at = (t % 8) * cps
-            worth = jnp.maximum(nets[slot][t // 8, at : at + cps], 0.0) * (before - now)
-            before = now
-            total = worth[:, :128]
-            for q in range(1, width // 128):
-                total = total + worth[:, q * 128 : (q + 1) * 128]
-            acc_ref[t * cps : (t + 1) * cps] += total
-
-    for k in range(CHUNKS):
-        with jax.named_scope(f"wait2_{k}"):
+    def weigh(tiles):
+        for g in range(0, cps, 8):
+            scale = ns_ref[g : g + 8]
+            before = []
+            for i, slot in tiles:
+                for q in range(width // 128):
+                    place = q * 128 // piece
+                    start = q * 128 % piece
+                    before.append(jnp.exp2(scale * st_ref[i * per_tile + place, 5:6, start : start + 128]))
+            for t in range(dates):
+                at = (t % 8) * cps + g
+                total = None
+                n = 0
+                for i, slot in tiles:
+                    for q in range(width // 128):
+                        lanes = slice(q * 128, (q + 1) * 128)
+                        now = jnp.exp2(scale * hazs[slot][t : t + 1, lanes])
+                        worth = jnp.maximum(nets[slot][t // 8, at : at + 8, lanes], 0.0) * (before[n] - now)
+                        before[n] = now
+                        n += 1
+                        total = worth if total is None else total + worth
+                acc_ref[t * cps + g : t * cps + g + 8] += total
+
+    def wait2(k):
+        with jax.named_scope("wait2"):
             all_of(s2_send, s2_recv, k, 6).wait_recv()
 
-        with jax.named_scope(f"weigh{k}"):
-
-            first = k * n_tm
-            prepare(first, 0)
-
-            @pl.loop(0, n_tm // 2)
-            def _(o):
-                i = first + 2 * o
-                prepare(i + 1, 1)
-                weigh(i, 0)
-                prepare(jnp.minimum(i + 2, first + n_tm - 1), 0)
-                weigh(i + 1, 1)
+    per_chunk = tiles // CHUNKS // 4
+    wait2(0)
+    prepare(0, 0)
+    prepare(1, 1)
+    with jax.named_scope("weigh"):
+
+        @pl.loop(0, tiles // 4)
+        def _(it):
+            k = it // per_chunk
+
+            @pl.when((it % per_chunk == 0) & (k + AHEAD < CHUNKS))
+            def _():
+                own(k + AHEAD)
+
+            @pl.when((it % per_chunk == per_chunk - 1) & (k + 1 < CHUNKS))
+            def _():
+                wait2(k + 1)
+
+            i = 4 * it
+            prepare(i + 2, 2)
+            prepare(i + 3, 3)
+            weigh([(i, 0), (i + 1, 1)])
+            j = jnp.minimum(i + 4, tiles - 2)
+            prepare(j, 0)
+            prepare(j + 1, 1)
+            weigh([(i + 2, 2), (i + 3, 3)])
 
     turned = jnp.sum(jnp.transpose(acc_ref[...]), axis=0, keepdims=True)
     part_ref[...] = turned * (1.0 / (total_paths * dt))
@@ -415,8 +448,8 @@
     dates, paths = shock_rate.shape
     ccys, cps = fx_vol.shape[0], hazard_scale.shape[0]
     geometry = (n_tm, n_path, paths, dates, cps, ccys, dates * n_tm, paths * n_path)
-    width = paths // (CHUNKS * n_tm)
-    tiles = CHUNKS * n_tm
+    width, piece = TILE, paths // (CHUNKS * n_tm)
+    tiles = paths // width
     count = trades[0].shape[0]
     vmem = functools.partial(pl.BlockSpec, memory_space=pltpu.VMEM)
     anywhere = functools.partial(pl.BlockSpec, memory_space=pl.ANY)
@@ -424,8 +457,8 @@
     profile, cva = pl.pallas_call(
         functools.partial(kernel, geometry),
         out_shape=(
-            jax.ShapeDtypeStruct((dates, cps), F32),
-            jax.ShapeDtypeStruct((1, cps), F32),
+            pltpu.VMEM((dates, cps), F32),
+            pltpu.VMEM((1, cps), F32),
         ),
         in_specs=[anywhere()] * 10,
         out_specs=(vmem(), vmem()),
@@ -434,10 +467,10 @@
             pltpu.VMEM((ccys, dates, paths), F32),
             pltpu.VMEM((tiles, 64, width), F32),
             pltpu.VMEM((tiles, 32, width), F32),
-            pltpu.VMEM((tiles, 8, width), F32),
-            pltpu.VMEM((CHUNKS, n_tm, 8, width), F32),
-            pltpu.VMEM((CHUNKS, n_tm, 8, width), F32),
-            pltpu.VMEM((tiles, 8, width), F32),
+            pltpu.VMEM((CHUNKS * n_tm, 8, piece), F32),
+            pltpu.VMEM((CHUNKS, n_tm, 8, piece), F32),
+            pltpu.VMEM((CHUNKS, n_tm, 8, piece), F32),
+            pltpu.VMEM((CHUNKS * n_tm, 8, piece), F32),
             pltpu.VMEM((96, 256), BF16),
             pltpu.VMEM((48, 128), BF16),
             pltpu.VMEM((2, 256, 256), BF16),
@@ -446,6 +479,10 @@
             pltpu.VMEM((cps, 128), F32),
             pltpu.VMEM((2, 256, width), F32),
             pltpu.VMEM((2, 256, width), F32),
+            pltpu.VMEM((2, 256, width), F32),
+            pltpu.VMEM((2, 256, width), F32),
+            pltpu.VMEM((dates, width), F32),
+            pltpu.VMEM((dates, width), F32),
             pltpu.VMEM((dates, width), F32),
             pltpu.VMEM((dates, width), F32),
             pltpu.VMEM((dates * cps, 128), F32),

time: 46.8 us -> 43.3 us (0.925)
  Pallas kernels: 43.5 us -> 41.5 us
  local copies, waits for them, and re-layouts: 2.43 us -> 1.11 us
    pallas_call x1, Pallas kernels: 43.5 us -> 41.5 us  [per_device(): pl.pallas_call(functools.partial(kernel, geometry), out_shape=(pltpu.VMEM...]
    unnamed x2, local copies, waits for them, and re-layouts: 2.43 us -> 1.11 us
where the time goes in v3:
time: 43.3 us; the launch traced here: 43.2 us
  Pallas kernels  41.5 us (96%)
  local copies, waits for them, and re-layouts  1.11 us (3%)
  between operations  0.64 us (1%)
    pallas_call x1, Pallas kernels, per_device(): pl.pallas_call(functools.partial(kernel, geometry), out_shape=(pltpu.VMEM...  41.5 us
    unnamed x2, local copies, waits for them, and re-layouts  1.11 us

profile of v3, /device:TPU:1, one launch (start us, length us, event | category | flops | bytes accessed | tf_op | source)
XLA Modules:
  0.0 43.2 jit_solution(10140650258553305452)
XLA Ops:
  0.6 41.5 %shard_map.113 = (f32[16,32]{1,0:T(8,128)S(1)}, f32[1,32]{1,0:T(1,128)S(1)}) custom-call(f32[16,16384]{1,0:T(8,128)} %rate_hbm.1, f32[4,16,16384]{2,1,0:T(8,128)} %fx_hbm.1, f32[4]{0:T(128)} %vol_hbm.1, f32[4]{0:T(128)} %corr_hbm.1, f32[32]{0:T(128)} %scale_hbm.1, s32[1,512]{1,0:T(1,128)} %bitcast.7, s32[1,512]{1,0:T(1,128)} %bitcast.8, s32[1,512]{1,0:T(1,128)} %bitcast.9, ...), custom_call_target="tpu_custom_call" | custom-call | tf_op jit(solution)/shard_map/pallas_call | solution.py:457
  42.1 0.6 %copy.14 = f32[16,32]{1,0:T(8,128)} copy(f32[16,32]{1,0:T(8,128)S(1)} %get-tuple-element.6) | data formatting | bytes 4096
  42.7 0.5 %copy.15 = f32[32]{0:T(128)} copy(f32[32]{0:T(128)S(1)} %bitcast.6) | data formatting | bytes 256

commit v4 on v3

--- a/solution.py
+++ b/solution.py
@@ -15,9 +15,9 @@
 RATE_SHIFT = 1.5
 LOG2E = 1.4426950408889634
 
-CHUNKS = 8
+SIZES = (1, 1, 2, 2, 2)
 TILE = 256
-AHEAD = 4
+CROWD = 8
 MESH = pl.DeviceIdType.MESH
 F32 = jnp.float32
 BF16 = jnp.bfloat16
@@ -29,6 +29,11 @@
     mid = rest.astype(BF16)
     low = (rest - mid.astype(F32)).astype(BF16)
     return high, mid, low
+
+
+def split2(x):
+    high = x.astype(BF16)
+    return high, (x - high.astype(F32)).astype(BF16)
 
 
 def iota(shape, dim):
@@ -65,16 +70,17 @@
     dt = HORIZON / total_dates
     decay = math.exp(-2.0 / total_dates)
     noise = math.sqrt(1.0 - decay * decay)
-    piece = paths // (CHUNKS * n_tm)
     width = TILE
     tiles = paths // width
-    per_tile = width // piece
-    group = chunk_paths = n_tm * piece
+    per_tile = width // 128
+    chunks = len(SIZES)
+    assert paths == 128 * n_tm * sum(SIZES)
+    first = [n_tm * sum(SIZES[:k]) for k in range(chunks + 1)]
     me = lax.axis_index("tm")
     my_path = lax.axis_index("path")
 
     def load_copies(k):
-        lanes = pl.ds(k * chunk_paths, chunk_paths)
+        lanes = pl.ds(first[k] * 128, (first[k + 1] - first[k]) * 128)
         return (
             pltpu.make_async_copy(rate_hbm.at[:, lanes], xr.at[:, lanes], in_sem.at[0, k]),
             pltpu.make_async_copy(fx_hbm.at[:, :, lanes], xf.at[:, :, lanes], in_sem.at[1, k]),
@@ -93,7 +99,7 @@
         copy.start()
     for copy in small:
         copy.start()
-    for k in range(1, CHUNKS):
+    for k in range(1, chunks):
         for copy in load_copies(k):
             copy.start()
 
@@ -106,19 +112,19 @@
             barrier, inc=1, device_id={"path": lax.rem(my_path + i, n_path)}, device_id_type=MESH
         )
 
-    r, c = iota((96, 256), 0), iota((96, 256), 1)
-    s = c - jnp.where(c >= 80, 80, 0) - jnp.where(c >= 160, 80, 0)
+    r, c = iota((96, 160), 0), iota((96, 160), 1)
+    s = c - jnp.where(c >= 80, 80, 0)
     in_ccy, in_date = (s >> 4) - 1, s & 15
     last = jnp.full_like(r, 15)
     out_ccy = jnp.where(r < 64, (r & 31) >> 3, jnp.where((r < 80) | (r == 80), -1, jnp.where(r < 85, r - 81, 9)))
     out_date = jnp.where(r < 64, ((r >> 5) << 3) + (r & 7), jnp.where(r < 80, r - 64, last))
-    m1_ref[...] = ones_where((c < 240) & (in_ccy == out_ccy) & (in_date <= out_date)).astype(BF16)
-    r, c = iota((48, 128), 0), iota((48, 128), 1)
+    m1_ref[...] = ones_where((in_ccy == out_ccy) & (in_date <= out_date)).astype(BF16)
+    r, c = iota((48, 64), 0), iota((48, 64), 1)
     s = c & 31
     in_kind, in_date = s >> 4, s & 15
     out_kind = jnp.where(r < 32, r >> 4, jnp.where(r == 37, 0, jnp.where(r == 38, 1, 9)))
     out_date = jnp.where(r < 32, r & 15, jnp.full_like(r, 15))
-    m2_ref[...] = ones_where((c < 96) & (in_kind == out_kind) & (in_date <= out_date)).astype(BF16)
+    m2_ref[...] = ones_where((in_kind == out_kind) & (in_date <= out_date)).astype(BF16)
 
     small[0].wait()
     small[1].wait()
@@ -132,45 +138,47 @@
     c_rate, c_own, c_drift = [], [], []
     for j in range(ccys):
         vol, corr = vec(vol_s, j), vec(corr_s, j)
-        c_rate.append(wide(vol * (LOG2E * math.sqrt(dt)) * corr, group))
-        c_own.append(wide(vol * (LOG2E * math.sqrt(dt)) * jnp.sqrt(1.0 - corr * corr), group))
-        c_drift.append(wide((0.5 * LOG2E * dt) * vol * vol, group))
+        c_rate.append(vol * (LOG2E * math.sqrt(dt)) * corr)
+        c_own.append(vol * (LOG2E * math.sqrt(dt)) * jnp.sqrt(1.0 - corr * corr))
+        c_drift.append((0.5 * LOG2E * dt) * vol * vol)
 
     def date_col(n):
         return iota((dates, n), 0).astype(F32)
 
     log_decay = -2.0 / total_dates
 
-    def walk(first):
-        lanes = pl.ds(pl.multiple_of(first, group), group)
+    def walk(k):
+        group = (first[k + 1] - first[k]) * 128
+        lanes = pl.ds(first[k] * 128, group)
         rate = xr[:, lanes]
         rows = [rate * (noise * jnp.exp(-log_decay * date_col(group)))]
         for j in range(ccys):
-            rows.append((c_rate[j] * rate + c_own[j] * xf[j, :, lanes]) - c_drift[j])
-        high, mid, low = split3(jnp.concatenate(rows, axis=0))
-        right = jnp.concatenate([high, mid, low, jnp.zeros((16, group), BF16)], axis=0)
+            rows.append((wide(c_rate[j], group) * rate + wide(c_own[j], group) * xf[j, :, lanes]) - wide(c_drift[j], group))
+        right = jnp.concatenate(split2(jnp.concatenate(rows, axis=0)), axis=0)
         out = jnp.dot(m1_ref[...], right, preferred_element_type=F32)
         power = jnp.exp(log_decay * date_col(group))
         shifted = out[64:80] * power + RATE_SHIFT
         cost = dt * (0.1 + 0.5 * shifted * shifted)
         slope = (dt * decay) * power * shifted
-        high, mid, low = split3(jnp.concatenate([cost, slope], axis=0))
-        right = jnp.concatenate([high, mid, low, jnp.zeros((32, group), BF16)], axis=0)
+        right = jnp.concatenate(split2(jnp.concatenate([cost, slope], axis=0)), axis=0)
         out2 = jnp.dot(m2_ref[...], right, preferred_element_type=F32)
         row = iota((8, group), 0)
         ends = jnp.where(row == 0, decay ** (dates - 1), 1.0) * out[80:88] + out2[32:40]
         for q in range(group // width):
             part = slice(q * width, (q + 1) * width)
-            log_ref[first // width + q] = out[:64, part]
-            ab_ref[first // width + q] = out2[:32, part]
-        for q in range(n_tm):
-            sum_ref[first // piece + q] = ends[:, q * piece : (q + 1) * piece]
+            log_ref[first[k] // per_tile + q] = out[:64, part]
+            ab_ref[first[k] // per_tile + q] = out2[:32, part]
+        for q in range(group // 128):
+            sum_ref[first[k] + q] = ends[:, q * 128 : (q + 1) * 128]
+
+    def columns(k, device):
+        return pl.ds(first[k] + device * SIZES[k], SIZES[k])
 
     def send1(k, i):
         owner = lax.rem(me + i, n_tm)
         return pltpu.make_async_remote_copy(
-            src_ref=sum_ref.at[k * n_tm + owner, pl.ds(0, 7)],
-            dst_ref=rcv_ref.at[k, me, pl.ds(0, 7)],
+            src_ref=sum_ref.at[columns(k, owner), pl.ds(0, 7)],
+            dst_ref=rcv_ref.at[columns(k, me), pl.ds(0, 7)],
             send_sem=s1_send.at[k],
             recv_sem=s1_recv.at[k],
             device_id={"tm": owner},
@@ -180,8 +188,8 @@
     def send2(k, i):
         block = lax.rem(me + i, n_tm)
         return pltpu.make_async_remote_copy(
-            src_ref=pre_ref.at[k, block, pl.ds(0, 6)],
-            dst_ref=st_ref.at[k * n_tm + me, pl.ds(0, 6)],
+            src_ref=pre_ref.at[columns(k, block), pl.ds(0, 6)],
+            dst_ref=st_ref.at[columns(k, me), pl.ds(0, 6)],
             send_sem=s2_send.at[k],
             recv_sem=s2_recv.at[k],
             device_id={"tm": block},
@@ -190,8 +198,8 @@
 
     def all_of(send, recv, k, rows):
         return pltpu.make_async_remote_copy(
-            src_ref=rcv_ref.at[k, pl.ds(0, n_tm - 1), pl.ds(0, rows)],
-            dst_ref=rcv_ref.at[k, pl.ds(0, n_tm - 1), pl.ds(0, rows)],
+            src_ref=rcv_ref.at[pl.ds(0, (n_tm - 1) * SIZES[k]), pl.ds(0, rows)],
+            dst_ref=rcv_ref.at[pl.ds(0, (n_tm - 1) * SIZES[k]), pl.ds(0, rows)],
             send_sem=send.at[k],
             recv_sem=recv.at[k],
             device_id={"tm": me},
@@ -203,7 +211,7 @@
             for copy in load_copies(k):
                 copy.wait()
         with jax.named_scope(f"walk{k}"):
-            walk(k * chunk_paths)
+            walk(k)
         if k == 0:
             with jax.named_scope("barrier"):
                 pl.semaphore_wait(barrier, n_tm - 1 + n_path - 1)
@@ -212,32 +220,29 @@
 
     block_gain = decay**dates
     block_square = 0.5 * dt * sum(decay ** (2 * (u + 1)) for u in range(dates))
-    kind = iota((8, piece), 0)
-    gain = jnp.where(kind == 0, block_gain, 1.0)
+    kind = iota((8, 128), 0)
 
     def own(k):
-        with jax.named_scope("wait1"):
+        with jax.named_scope(f"wait1_{k}"):
             all_of(s1_send, s1_recv, k, 7).wait_recv()
-        rcv_ref[k, me] = sum_ref[k * n_tm + me]
-        state = jnp.zeros((8, piece), F32)
-        for b in range(n_tm):
-            pre_ref[k, b] = state
-            if b < n_tm - 1:
-                x = rcv_ref[k, b]
-                rate = jnp.broadcast_to(state[0:1], (8, piece))
-                slope = jnp.broadcast_to(x[6:7], (8, piece))
-                extra = rate * (slope + rate * block_square)
-                state = gain * state + jnp.where(kind < 6, x, 0.0) + jnp.where(kind == 5, extra, 0.0)
+        rcv_ref[columns(k, me)] = sum_ref[columns(k, me)]
+        for q in range(SIZES[k]):
+            rate = rest = jnp.zeros((8, 128), F32)
+            for b in range(n_tm):
+                at = first[k] + b * SIZES[k] + q
+                pre_ref[at] = jnp.where(kind == 0, rate, rest)
+                if b < n_tm - 1:
+                    x = rcv_ref[at]
+                    slope = jnp.broadcast_to(x[6:7], (8, 128))
+                    rest = rest + (x + jnp.where(kind == 5, rate * (slope + rate * block_square), 0.0))
+                    rate = block_gain * rate + jnp.broadcast_to(x[0:1], (8, 128))
         for i in tm_order(n_tm):
             send2(k, i).start()
-        st_ref[k * n_tm + me] = pre_ref[k, me]
-
-    for k in range(6):
+        st_ref[columns(k, me)] = pre_ref[columns(k, me)]
+
+    for k in range(chunks):
         walk_and_send(k)
     own(0)
-    walk_and_send(6)
-    own(1)
-    walk_and_send(7)
 
     for copy in small[2:]:
         copy.wait()
@@ -254,16 +259,16 @@
     col = iota((256, trades), 0)
     pick = jnp.concatenate(
         [
-            ones_where((col < 192) & (ccy == ((col & 31) >> 3))).astype(BF16),
-            ones_where((col >= 192) & (col < 195)).astype(BF16),
+            ones_where((col < 160) & (ccy == ((col & 31) >> 3))).astype(BF16),
+            ones_where((col >= 160) & (col < 163)).astype(BF16),
         ],
         axis=1,
     )
     r, c = iota((256, 256), 0), iota((256, 256), 1)
-    keep = (c >= 192) | ((r >> 5) == (c & 7))
+    keep = (c >= 160) | ((r >> 5) == (c & 7))
     part = c >> 5
-    is_high = (part == 0) | (part == 3) | (part == 5) | (c == 192)
-    is_mid = (part == 1) | (part == 4) | (c == 193)
+    is_high = (part == 0) | (part == 3) | (c == 160)
+    is_mid = (part == 1) | (part == 4) | (c == 161)
     for half in range(2):
         blocks = []
         for t in range(half * 8, half * 8 + 8):
@@ -283,22 +288,23 @@
             )
         high, mid, low = split3(jnp.where(keep, table, 0.0))
         chosen = jnp.where(is_high, high.astype(F32), jnp.where(is_mid, mid.astype(F32), low.astype(F32)))
-        lhs_ref[half] = chosen.astype(BF16)
+        lhs_ref[half] = chosen.astype(BF16)[:, :176]
 
     row = iota((cps, 128), 0)
     ns = jnp.zeros((cps, 128), F32)
     for q in range(cps):
         ns = jnp.where(row == q, scale_s[q] * (-LOG2E), ns)
-    ns_ref[...] = ns
+    for t in range(dates):
+        ns_ref[t] = ns
     acc_ref[...] = jnp.zeros_like(acc_ref)
 
-    own(2)
-    own(3)
+    for k in range(1, chunks):
+        own(k)
 
     squares = 0.5 * dt * jnp.exp(2 * log_decay) * (1.0 - jnp.exp(2 * log_decay * (date_col(width) + 1.0))) * (
         1.0 / (1.0 - math.exp(2 * log_decay))
     )
-    fill = ones_where(iota((64, width), 0) < 16).astype(BF16)
+    fill = jnp.ones((16, width), BF16)
 
     nets, hazs = (net0_ref, net1_ref, net2_ref, net3_ref), (haz0_ref, haz1_ref, haz2_ref, haz3_ref)
 
@@ -312,19 +318,17 @@
             for j in range(ccys):
                 at = half * 32 + j * 8
                 spots.append(jnp.exp2(log_ref[i, at : at + 8] + state[1 + j : 2 + j]))
-            high, mid, low = split3(jnp.concatenate(spots, axis=0))
-            right = jnp.concatenate([high, high, high, mid, mid, low, fill], axis=0)
+            high, mid = split2(jnp.concatenate(spots, axis=0))
+            right = jnp.concatenate([high, high, high, mid, mid, fill], axis=0)
             nets[slot][half] = jnp.dot(lhs_ref[half], right, preferred_element_type=F32)
 
     def weigh(tiles):
-        for g in range(0, cps, 8):
-            scale = ns_ref[g : g + 8]
+        for g in range(0, cps, CROWD):
+            scale = ns_ref[0, g : g + CROWD]
             before = []
             for i, slot in tiles:
                 for q in range(width // 128):
-                    place = q * 128 // piece
-                    start = q * 128 % piece
-                    before.append(jnp.exp2(scale * st_ref[i * per_tile + place, 5:6, start : start + 128]))
+                    before.append(jnp.exp2(scale * st_ref[i * per_tile + q, 5:6]))
             for t in range(dates):
                 at = (t % 8) * cps + g
                 total = None
@@ -332,18 +336,17 @@
                 for i, slot in tiles:
                     for q in range(width // 128):
                         lanes = slice(q * 128, (q + 1) * 128)
-                        now = jnp.exp2(scale * hazs[slot][t : t + 1, lanes])
-                        worth = jnp.maximum(nets[slot][t // 8, at : at + 8, lanes], 0.0) * (before[n] - now)
+                        now = jnp.exp2(ns_ref[t, g : g + CROWD] * hazs[slot][t : t + 1, lanes])
+                        worth = jnp.maximum(nets[slot][t // 8, at : at + CROWD, lanes], 0.0) * (before[n] - now)
                         before[n] = now
                         n += 1
                         total = worth if total is None else total + worth
-                acc_ref[t * cps + g : t * cps + g + 8] += total
+                acc_ref[t * cps + g : t * cps + g + CROWD] += total
 
     def wait2(k):
-        with jax.named_scope("wait2"):
+        with jax.named_scope(f"wait2_{k}"):
             all_of(s2_send, s2_recv, k, 6).wait_recv()
 
-    per_chunk = tiles // CHUNKS // 4
     wait2(0)
     prepare(0, 0)
     prepare(1, 1)
@@ -351,15 +354,11 @@
 
         @pl.loop(0, tiles // 4)
         def _(it):
-            k = it // per_chunk
-
-            @pl.when((it % per_chunk == 0) & (k + AHEAD < CHUNKS))
-            def _():
-                own(k + AHEAD)
-
-            @pl.when((it % per_chunk == per_chunk - 1) & (k + 1 < CHUNKS))
-            def _():
-                wait2(k + 1)
+            for k in range(1, chunks):
+
+                @pl.when(it == first[k] // per_tile // 4 - 1)
+                def _():
+                    wait2(k)
 
             i = 4 * it
             prepare(i + 2, 2)
@@ -431,7 +430,7 @@
     for i in tm_order(n_tm):
         send_cva(i).start()
 
-    for k in range(CHUNKS):
+    for k in range(chunks):
         all_of(s1_send, s1_recv, k, 7).wait_send()
         all_of(s2_send, s2_recv, k, 6).wait_send()
     all_parts(parts_rcv, n_path, 0, {"path": my_path}).wait_send()
@@ -444,12 +443,23 @@
     all_parts(cparts_rcv, n_tm, 1, {"tm": me}).wait_send()
 
 
+def hand_out(profile, cva, profile_out, cva_out, sems):
+    copies = [
+        pltpu.make_async_copy(profile, profile_out, sems.at[0]),
+        pltpu.make_async_copy(cva, cva_out, sems.at[1]),
+    ]
+    for copy in copies:
+        copy.start()
+    for copy in copies:
+        copy.wait()
+
+
 def per_device(n_tm, n_path, shock_rate, shock_fx, fx_vol, fx_corr, hazard_scale, *trades):
     dates, paths = shock_rate.shape
     ccys, cps = fx_vol.shape[0], hazard_scale.shape[0]
     geometry = (n_tm, n_path, paths, dates, cps, ccys, dates * n_tm, paths * n_path)
-    width, piece = TILE, paths // (CHUNKS * n_tm)
-    tiles = paths // width
+    width = TILE
+    tiles, columns, chunks = paths // width, paths // 128, len(SIZES)
     count = trades[0].shape[0]
     vmem = functools.partial(pl.BlockSpec, memory_space=pltpu.VMEM)
     anywhere = functools.partial(pl.BlockSpec, memory_space=pl.ANY)
@@ -467,16 +477,16 @@
             pltpu.VMEM((ccys, dates, paths), F32),
             pltpu.VMEM((tiles, 64, width), F32),
             pltpu.VMEM((tiles, 32, width), F32),
-            pltpu.VMEM((CHUNKS * n_tm, 8, piece), F32),
-            pltpu.VMEM((CHUNKS, n_tm, 8, piece), F32),
-            pltpu.VMEM((CHUNKS, n_tm, 8, piece), F32),
-            pltpu.VMEM((CHUNKS * n_tm, 8, piece), F32),
-            pltpu.VMEM((96, 256), BF16),
-            pltpu.VMEM((48, 128), BF16),
-            pltpu.VMEM((2, 256, 256), BF16),
+            pltpu.VMEM((columns, 8, 128), F32),
+            pltpu.VMEM((columns, 8, 128), F32),
+            pltpu.VMEM((columns, 8, 128), F32),
+            pltpu.VMEM((columns, 8, 128), F32),
+            pltpu.VMEM((96, 160), BF16),
+            pltpu.VMEM((48, 64), BF16),
+            pltpu.VMEM((2, 256, 176), BF16),
             pltpu.VMEM((dates, count), F32),
             pltpu.VMEM((dates, count), F32),
-            pltpu.VMEM((cps, 128), F32),
+            pltpu.VMEM((dates, cps, 128), F32),
             pltpu.VMEM((2, 256, width), F32),
             pltpu.VMEM((2, 256, width), F32),
             pltpu.VMEM((2, 256, width), F32),
@@ -498,17 +508,24 @@
             pltpu.VMEM((1, count), jnp.int32),
             pltpu.VMEM((1, count), F32),
             pltpu.VMEM((1, count), F32),
-            sems((2, CHUNKS)),
+            sems((2, chunks)),
             sems((8,)),
-            sems((CHUNKS,)),
-            sems((CHUNKS,)),
-            sems((CHUNKS,)),
-            sems((CHUNKS,)),
+            sems((chunks,)),
+            sems((chunks,)),
+            sems((chunks,)),
+            sems((chunks,)),
             sems((2,)),
             sems((2,)),
         ],
         compiler_params=pltpu.CompilerParams(collective_id=0, has_side_effects=True),
     )(shock_rate, shock_fx, fx_vol, fx_corr, hazard_scale, *(a.reshape(1, count) for a in trades))
+    profile, cva = pl.pallas_call(
+        hand_out,
+        out_shape=(jax.ShapeDtypeStruct((dates, cps), F32), jax.ShapeDtypeStruct((1, cps), F32)),
+        in_specs=[vmem(), vmem()],
+        out_specs=(anywhere(), anywhere()),
+        scratch_shapes=[sems((2,))],
+    )(*(pltpu.with_memory_space_constraint(a, pltpu.VMEM) for a in (profile, cva)))
     return profile, cva.reshape(cps)
 
 

time: 43.3 us -> 41.3 us (0.954)
  local copies, waits for them, and re-layouts: 1.11 us -> 0 us
  Pallas kernels: 41.5 us -> 40.6 us
    pallas_call x1, Pallas kernels: 41.5 us -> 40 us  [per_device(): pl.pallas_call(functools.partial(kernel, geometry), out_shape=(pltpu.VMEM...]
    unnamed x2 -> x0, local copies, waits for them, and re-layouts: 1.11 us -> none
    pallas_call x0 -> x1, Pallas kernels: none -> 0.62 us  [per_device(): pl.pallas_call(hand_out, out_shape=(jax.ShapeDtypeStruct((dates, cps), F3...]
where the time goes in v4:
time: 41.3 us
  Pallas kernels  40.6 us (98%)
  between operations  0.64 us (2%)
    pallas_call x1, Pallas kernels, per_device(): pl.pallas_call(functools.partial(kernel, geometry), out_shape=(pltpu.VMEM...  40 us

profile of v4, /device:TPU:1, one launch (start us, length us, event | category | flops | bytes accessed | tf_op | source)
XLA Modules:
  0.0 41.3 jit_solution(17035179443105009402)
XLA Ops:
  0.6 40.0 %shard_map.113 = (f32[16,32]{1,0:T(8,128)S(1)}, f32[1,32]{1,0:T(1,128)S(1)}) custom-call(f32[16,16384]{1,0:T(8,128)} %rate_hbm.1, f32[4,16,16384]{2,1,0:T(8,128)} %fx_hbm.1, f32[4]{0:T(128)} %vol_hbm.1, f32[4]{0:T(128)} %corr_hbm.1, f32[32]{0:T(128)} %scale_hbm.1, s32[1,512]{1,0:T(1,128)} %bitcast.6, s32[1,512]{1,0:T(1,128)} %bitcast.7, s32[1,512]{1,0:T(1,128)} %bitcast.8, ...), custom_call_target="tpu_custom_call" | custom-call | tf_op jit(solution)/shard_map/pallas_call | solution.py:467
  40.6 0.6 %shard_map.114 = (f32[16,32]{1,0:T(8,128)}, f32[1,32]{1,0:T(1,128)}) custom-call(f32[16,32]{1,0:T(8,128)S(1)} %get-tuple-element.6.profile, f32[1,32]{1,0:T(1,128)S(1)} %get-tuple-element.7.cva), custom_call_target="tpu_custom_call" | custom-call | tf_op jit(solution)/shard_map/pallas_call | solution.py:522

commit v5 on v4

--- a/solution.py
+++ b/solution.py
@@ -112,6 +112,9 @@
             barrier, inc=1, device_id={"path": lax.rem(my_path + i, n_path)}, device_id_type=MESH
         )
 
+    small[0].wait()
+    small[1].wait()
+
     r, c = iota((96, 160), 0), iota((96, 160), 1)
     s = c - jnp.where(c >= 80, 80, 0)
     in_ccy, in_date = (s >> 4) - 1, s & 15
@@ -125,9 +128,6 @@
     out_kind = jnp.where(r < 32, r >> 4, jnp.where(r == 37, 0, jnp.where(r == 38, 1, 9)))
     out_date = jnp.where(r < 32, r & 15, jnp.full_like(r, 15))
     m2_ref[...] = ones_where((in_kind == out_kind) & (in_date <= out_date)).astype(BF16)
-
-    small[0].wait()
-    small[1].wait()
 
     def vec(ref, j):
         return jnp.full((1, 128), ref[j], F32)
@@ -240,10 +240,8 @@
             send2(k, i).start()
         st_ref[columns(k, me)] = pre_ref[columns(k, me)]
 
-    for k in range(chunks):
+    for k in range(chunks - 1):
         walk_and_send(k)
-    own(0)
-
     for copy in small[2:]:
         copy.wait()
 
@@ -298,7 +296,11 @@
         ns_ref[t] = ns
     acc_ref[...] = jnp.zeros_like(acc_ref)
 
-    for k in range(1, chunks):
+    own(0)
+    own(1)
+    walk_and_send(chunks - 1)
+
+    for k in range(2, chunks - 1):
         own(k)
 
     squares = 0.5 * dt * jnp.exp(2 * log_decay) * (1.0 - jnp.exp(2 * log_decay * (date_col(width) + 1.0))) * (
@@ -352,14 +354,7 @@
     prepare(1, 1)
     with jax.named_scope("weigh"):
 
-        @pl.loop(0, tiles // 4)
-        def _(it):
-            for k in range(1, chunks):
-
-                @pl.when(it == first[k] // per_tile // 4 - 1)
-                def _():
-                    wait2(k)
-
+        def step(it):
             i = 4 * it
             prepare(i + 2, 2)
             prepare(i + 3, 3)
@@ -368,6 +363,16 @@
             prepare(j, 0)
             prepare(j + 1, 1)
             weigh([(i + 2, 2), (i + 3, 3)])
+
+        begin = 0
+        for k in range(1, chunks + 1):
+            end = first[k] // per_tile // 4 - (k < chunks)
+            pl.loop(begin, end)(step)
+            begin = end
+            if k == 2:
+                own(chunks - 1)
+            if k < chunks:
+                wait2(k)
 
     turned = jnp.sum(jnp.transpose(acc_ref[...]), axis=0, keepdims=True)
     part_ref[...] = turned * (1.0 / (total_paths * dt))

time: 41.3 us -> 40.8 us (0.988)
  Pallas kernels: 40.6 us -> 40.1 us
    pallas_call x1, Pallas kernels: 40 us -> 39.5 us  [per_device(): pl.pallas_call(functools.partial(kernel, geometry), out_shape=(pltpu.VMEM...]
where the time goes in v5:
time: 40.8 us; the launch traced here: 40.7 us
  Pallas kernels  40.1 us (98%)
  between operations  0.64 us (2%)
    pallas_call x1, Pallas kernels, per_device(): pl.pallas_call(functools.partial(kernel, geometry), out_shape=(pltpu.VMEM...  39.5 us

profile of v5, /device:TPU:1, one launch (start us, length us, event | category | flops | bytes accessed | tf_op | source)
XLA Modules:
  0.0 40.7 jit_solution(8011594609972241221)
XLA Ops:
  0.6 39.5 %shard_map.113 = (f32[16,32]{1,0:T(8,128)S(1)}, f32[1,32]{1,0:T(1,128)S(1)}) custom-call(f32[16,16384]{1,0:T(8,128)} %rate_hbm.1, f32[4,16,16384]{2,1,0:T(8,128)} %fx_hbm.1, f32[4]{0:T(128)} %vol_hbm.1, f32[4]{0:T(128)} %corr_hbm.1, f32[32]{0:T(128)} %scale_hbm.1, s32[1,512]{1,0:T(1,128)} %bitcast.6, s32[1,512]{1,0:T(1,128)} %bitcast.7, s32[1,512]{1,0:T(1,128)} %bitcast.8, ...), custom_call_target="tpu_custom_call" | custom-call | tf_op jit(solution)/shard_map/pallas_call | solution.py:472
  40.1 0.6 %shard_map.114 = (f32[16,32]{1,0:T(8,128)}, f32[1,32]{1,0:T(1,128)}) custom-call(f32[16,32]{1,0:T(8,128)S(1)} %get-tuple-element.6.profile, f32[1,32]{1,0:T(1,128)S(1)} %get-tuple-element.7.cva), custom_call_target="tpu_custom_call" | custom-call | tf_op jit(solution)/shard_map/pallas_call | solution.py:527

commit v6 on v5

--- a/solution.py
+++ b/solution.py
@@ -78,6 +78,8 @@
     first = [n_tm * sum(SIZES[:k]) for k in range(chunks + 1)]
     me = lax.axis_index("tm")
     my_path = lax.axis_index("path")
+    near = lax.rem(my_path, 2)
+    near_path, far_path = my_path + 1 - near, my_path - near
 
     def load_copies(k):
         lanes = pl.ds(first[k] * 128, (first[k + 1] - first[k]) * 128)
@@ -107,6 +109,12 @@
 
     for i in tm_order(n_tm):
         pl.semaphore_signal(barrier, inc=1, device_id={"tm": lax.rem(me + i, n_tm)}, device_id_type=MESH)
+        pl.semaphore_signal(
+            barrier,
+            inc=1,
+            device_id={"tm": lax.rem(me + i, n_tm), "path": near_path + far_path - my_path},
+            device_id_type=MESH,
+        )
     for i in path_order(n_path):
         pl.semaphore_signal(
             barrier, inc=1, device_id={"path": lax.rem(my_path + i, n_path)}, device_id_type=MESH
@@ -178,33 +186,33 @@
         owner = lax.rem(me + i, n_tm)
         return pltpu.make_async_remote_copy(
             src_ref=sum_ref.at[columns(k, owner), pl.ds(0, 7)],
-            dst_ref=rcv_ref.at[columns(k, me), pl.ds(0, 7)],
+            dst_ref=rcv_ref.at[near, columns(k, me), pl.ds(0, 7)],
             send_sem=s1_send.at[k],
-            recv_sem=s1_recv.at[k],
-            device_id={"tm": owner},
+            recv_sem=s1_recv.at[near, k],
+            device_id={"tm": owner, "path": near_path},
             device_id_type=MESH,
         )
 
-    def send2(k, i):
+    def send2(core, k, i):
         block = lax.rem(me + i, n_tm)
         return pltpu.make_async_remote_copy(
-            src_ref=pre_ref.at[columns(k, block), pl.ds(0, 6)],
+            src_ref=pre_ref.at[core, columns(k, block), pl.ds(0, 6)],
             dst_ref=st_ref.at[columns(k, me), pl.ds(0, 6)],
-            send_sem=s2_send.at[k],
+            send_sem=s2_send.at[core, k],
             recv_sem=s2_recv.at[k],
-            device_id={"tm": block},
+            device_id={"tm": block, "path": far_path + core},
             device_id_type=MESH,
         )
 
-    def all_of(send, recv, k, rows):
+    def all_of(send, recv, k, rows, count):
+        part = rcv_ref.at[0, pl.ds(0, count * SIZES[k]), pl.ds(0, rows)]
         return pltpu.make_async_remote_copy(
-            src_ref=rcv_ref.at[pl.ds(0, (n_tm - 1) * SIZES[k]), pl.ds(0, rows)],
-            dst_ref=rcv_ref.at[pl.ds(0, (n_tm - 1) * SIZES[k]), pl.ds(0, rows)],
-            send_sem=send.at[k],
-            recv_sem=recv.at[k],
-            device_id={"tm": me},
-            device_id_type=MESH,
-        )
+            src_ref=part, dst_ref=part, send_sem=send, recv_sem=recv, device_id={"tm": me}, device_id_type=MESH
+        )
+
+    def each_core(act):
+        pl.when(near == 1)(lambda: act(n_tm - 1))
+        pl.when(near == 0)(lambda: act(n_tm))
 
     def walk_and_send(k):
         with jax.named_scope(f"inwait{k}"):
@@ -214,31 +222,44 @@
             walk(k)
         if k == 0:
             with jax.named_scope("barrier"):
-                pl.semaphore_wait(barrier, n_tm - 1 + n_path - 1)
+                pl.semaphore_wait(barrier, 2 * (n_tm - 1) + n_path - 1)
         for i in tm_order(n_tm):
             send1(k, i).start()
+
+        @pl.when(near == 0)
+        def _():
+            send1(k, 0).start()
 
     block_gain = decay**dates
     block_square = 0.5 * dt * sum(decay ** (2 * (u + 1)) for u in range(dates))
     kind = iota((8, 128), 0)
 
-    def own(k):
-        with jax.named_scope(f"wait1_{k}"):
-            all_of(s1_send, s1_recv, k, 7).wait_recv()
-        rcv_ref[columns(k, me)] = sum_ref[columns(k, me)]
+    def order(core, k):
         for q in range(SIZES[k]):
             rate = rest = jnp.zeros((8, 128), F32)
             for b in range(n_tm):
                 at = first[k] + b * SIZES[k] + q
-                pre_ref[at] = jnp.where(kind == 0, rate, rest)
+                pre_ref[core, at] = jnp.where(kind == 0, rate, rest)
                 if b < n_tm - 1:
-                    x = rcv_ref[at]
+                    x = rcv_ref[core, at]
                     slope = jnp.broadcast_to(x[6:7], (8, 128))
                     rest = rest + (x + jnp.where(kind == 5, rate * (slope + rate * block_square), 0.0))
                     rate = block_gain * rate + jnp.broadcast_to(x[0:1], (8, 128))
-        for i in tm_order(n_tm):
-            send2(k, i).start()
-        st_ref[columns(k, me)] = pre_ref[columns(k, me)]
+
+    def own(k):
+        @pl.when(near == 1)
+        def _():
+            with jax.named_scope(f"wait1_{k}"):
+                all_of(s1_send.at[k], s1_recv.at[0, k], k, 7, n_tm).wait_recv()
+            order(0, k)
+            for i in tm_order(n_tm) + [0]:
+                send2(0, k, i).start()
+            all_of(s1_send.at[k], s1_recv.at[1, k], k, 7, n_tm - 1).wait_recv()
+            rcv_ref[1, columns(k, me)] = sum_ref[columns(k, me)]
+            order(1, k)
+            for i in tm_order(n_tm):
+                send2(1, k, i).start()
+            st_ref[columns(k, me)] = pre_ref[1, columns(k, me)]
 
     for k in range(chunks - 1):
         walk_and_send(k)
@@ -347,7 +368,7 @@
 
     def wait2(k):
         with jax.named_scope(f"wait2_{k}"):
-            all_of(s2_send, s2_recv, k, 6).wait_recv()
+            each_core(lambda n: all_of(s1_send.at[k], s2_recv.at[k], k, 6, n).wait_recv())
 
     wait2(0)
     prepare(0, 0)
@@ -421,23 +442,32 @@
     cpart_ref[...] = total
     cparts_rcv[me] = total
 
-    def send_cva(i):
+    def send_cva(core, i):
         to = lax.rem(me + i, n_tm)
         return pltpu.make_async_remote_copy(
             src_ref=cpart_ref,
             dst_ref=cparts_rcv.at[me],
             send_sem=t_send.at[1],
             recv_sem=t_recv.at[1],
-            device_id={"tm": to},
+            device_id={"tm": to, "path": far_path + core},
             device_id_type=MESH,
         )
 
-    for i in tm_order(n_tm):
-        send_cva(i).start()
+    @pl.when(near == 1)
+    def _():
+        for i in tm_order(n_tm):
+            send_cva(0, i).start()
+            send_cva(1, i).start()
+
 
     for k in range(chunks):
-        all_of(s1_send, s1_recv, k, 7).wait_send()
-        all_of(s2_send, s2_recv, k, 6).wait_send()
+        each_core(lambda n: all_of(s1_send.at[k], s1_recv.at[0, k], k, 7, n).wait_send())
+
+        @pl.when(near == 1)
+        def _():
+            all_of(s2_send.at[0, k], s1_recv.at[0, k], k, 6, n_tm).wait_send()
+            all_of(s2_send.at[1, k], s1_recv.at[0, k], k, 6, n_tm - 1).wait_send()
+
     all_parts(parts_rcv, n_path, 0, {"path": my_path}).wait_send()
     with jax.named_scope("wait_t2"):
         all_parts(cparts_rcv, n_tm, 1, {"tm": me}).wait_recv()
@@ -445,7 +475,11 @@
     for q in range(1, n_tm):
         cva = cva + cparts_rcv[q]
     cva_out[...] = cva[:, :cps]
-    all_parts(cparts_rcv, n_tm, 1, {"tm": me}).wait_send()
+
+    @pl.when(near == 1)
+    def _():
+        all_parts(cparts_rcv, n_tm, 1, {"tm": me}).wait_send()
+        all_parts(cparts_rcv, n_tm, 1, {"tm": me}).wait_send()
 
 
 def hand_out(profile, cva, profile_out, cva_out, sems):
@@ -483,8 +517,8 @@
             pltpu.VMEM((tiles, 64, width), F32),
             pltpu.VMEM((tiles, 32, width), F32),
             pltpu.VMEM((columns, 8, 128), F32),
-            pltpu.VMEM((columns, 8, 128), F32),
-            pltpu.VMEM((columns, 8, 128), F32),
+            pltpu.VMEM((2, columns, 8, 128), F32),
+            pltpu.VMEM((2, columns, 8, 128), F32),
             pltpu.VMEM((columns, 8, 128), F32),
             pltpu.VMEM((96, 160), BF16),
             pltpu.VMEM((48, 64), BF16),
@@ -516,8 +550,8 @@
             sems((2, chunks)),
             sems((8,)),
             sems((chunks,)),
-            sems((chunks,)),
-            sems((chunks,)),
+            sems((2, chunks)),
+            sems((2, chunks)),
             sems((chunks,)),
             sems((2,)),
             sems((2,)),

time: 40.8 us -> 39.9 us (0.978)
  Pallas kernels: 40.1 us -> 39.2 us
    pallas_call x1, Pallas kernels: 39.5 us -> 38.6 us  [per_device(): pl.pallas_call(functools.partial(kernel, geometry), out_shape=(pltpu.VMEM...]
where the time goes in v6:
time: 39.9 us
  Pallas kernels  39.2 us (98%)
  between operations  0.64 us (2%)
    pallas_call x1, Pallas kernels, per_device(): pl.pallas_call(functools.partial(kernel, geometry), out_shape=(pltpu.VMEM...  38.6 us

profile of v6, /device:TPU:1, one launch (start us, length us, event | category | flops | bytes accessed | tf_op | source)
XLA Modules:
  0.0 39.9 jit_solution(4684725403877855427)
XLA Ops:
  0.6 38.6 %shard_map.113 = (f32[16,32]{1,0:T(8,128)S(1)}, f32[1,32]{1,0:T(1,128)S(1)}) custom-call(f32[16,16384]{1,0:T(8,128)} %rate_hbm.1, f32[4,16,16384]{2,1,0:T(8,128)} %fx_hbm.1, f32[4]{0:T(128)} %vol_hbm.1, f32[4]{0:T(128)} %corr_hbm.1, f32[32]{0:T(128)} %scale_hbm.1, s32[1,512]{1,0:T(1,128)} %bitcast.6, s32[1,512]{1,0:T(1,128)} %bitcast.7, s32[1,512]{1,0:T(1,128)} %bitcast.8, ...), custom_call_target="tpu_custom_call" | custom-call | tf_op jit(solution)/shard_map/pallas_call | solution.py:506
  39.2 0.6 %shard_map.114 = (f32[16,32]{1,0:T(8,128)}, f32[1,32]{1,0:T(1,128)}) custom-call(f32[16,32]{1,0:T(8,128)S(1)} %get-tuple-element.6.profile, f32[1,32]{1,0:T(1,128)S(1)} %get-tuple-element.7.cva), custom_call_target="tpu_custom_call" | custom-call | tf_op jit(solution)/shard_map/pallas_call | solution.py:561

commit v7 on v6

--- a/solution.py
+++ b/solution.py
@@ -108,16 +108,16 @@
     barrier = pltpu.get_barrier_semaphore()
 
     for i in tm_order(n_tm):
-        pl.semaphore_signal(barrier, inc=1, device_id={"tm": lax.rem(me + i, n_tm)}, device_id_type=MESH)
+        pl.semaphore_signal(barrier, inc=1, device_id={"tm": ((me + i) & (n_tm - 1))}, device_id_type=MESH)
         pl.semaphore_signal(
             barrier,
             inc=1,
-            device_id={"tm": lax.rem(me + i, n_tm), "path": near_path + far_path - my_path},
+            device_id={"tm": ((me + i) & (n_tm - 1)), "path": near_path + far_path - my_path},
             device_id_type=MESH,
         )
     for i in path_order(n_path):
         pl.semaphore_signal(
-            barrier, inc=1, device_id={"path": lax.rem(my_path + i, n_path)}, device_id_type=MESH
+            barrier, inc=1, device_id={"path": ((my_path + i) & (n_path - 1))}, device_id_type=MESH
         )
 
     small[0].wait()
@@ -183,7 +183,7 @@
         return pl.ds(first[k] + device * SIZES[k], SIZES[k])
 
     def send1(k, i):
-        owner = lax.rem(me + i, n_tm)
+        owner = ((me + i) & (n_tm - 1))
         return pltpu.make_async_remote_copy(
             src_ref=sum_ref.at[columns(k, owner), pl.ds(0, 7)],
             dst_ref=rcv_ref.at[near, columns(k, me), pl.ds(0, 7)],
@@ -194,7 +194,7 @@
         )
 
     def send2(core, k, i):
-        block = lax.rem(me + i, n_tm)
+        block = ((me + i) & (n_tm - 1))
         return pltpu.make_async_remote_copy(
             src_ref=pre_ref.at[core, columns(k, block), pl.ds(0, 6)],
             dst_ref=st_ref.at[columns(k, me), pl.ds(0, 6)],
@@ -388,7 +388,11 @@
         begin = 0
         for k in range(1, chunks + 1):
             end = first[k] // per_tile // 4 - (k < chunks)
-            pl.loop(begin, end)(step)
+            even = begin + (end - begin) // 2 * 2
+            if even > begin:
+                pl.loop(begin, even, unroll=2)(step)
+            if even < end:
+                step(even)
             begin = end
             if k == 2:
                 own(chunks - 1)
@@ -400,7 +404,7 @@
     parts_rcv[my_path] = part_ref[...]
 
     def send_part(i):
-        to = lax.rem(my_path + i, n_path)
+        to = ((my_path + i) & (n_path - 1))
         return pltpu.make_async_remote_copy(
             src_ref=part_ref,
             dst_ref=parts_rcv.at[my_path],
@@ -431,8 +435,6 @@
     profile = parts_rcv[0]
     for q in range(1, n_path):
         profile = profile + parts_rcv[q]
-    for t in range(dates):
-        prof_out[t : t + 1] = profile[:, t * cps : (t + 1) * cps]
     terms = profile * discount
     total = terms[:, :128]
     for q in range(1, dates * cps // 128):
@@ -443,7 +445,7 @@
     cparts_rcv[me] = total
 
     def send_cva(core, i):
-        to = lax.rem(me + i, n_tm)
+        to = ((me + i) & (n_tm - 1))
         return pltpu.make_async_remote_copy(
             src_ref=cpart_ref,
             dst_ref=cparts_rcv.at[me],
@@ -458,6 +460,9 @@
         for i in tm_order(n_tm):
             send_cva(0, i).start()
             send_cva(1, i).start()
+
+    for t in range(dates):
+        prof_out[t : t + 1] = profile[:, t * cps : (t + 1) * cps]
 
 
     for k in range(chunks):

time: 39.9 us -> 39.6 us (level)
  Pallas kernels: 39.2 us -> 38.7 us
    pallas_call x1, Pallas kernels: 38.6 us -> 38.1 us  [per_device(): pl.pallas_call(functools.partial(kernel, geometry), out_shape=(pltpu.VMEM...]
where the time goes in v7:
time: 39.6 us; the launch traced here: 39.5 us
  Pallas kernels  38.7 us (98%)
  between operations  0.8 us (2%)
    pallas_call x1, Pallas kernels, per_device(): pl.pallas_call(functools.partial(kernel, geometry), out_shape=(pltpu.VMEM...  38.1 us

profile of v7, /device:TPU:1, one launch (start us, length us, event | category | flops | bytes accessed | tf_op | source)
XLA Modules:
  0.0 39.5 jit_solution(11787597184069280895)
XLA Ops:
  0.6 38.1 %shard_map.113 = (f32[16,32]{1,0:T(8,128)S(1)}, f32[1,32]{1,0:T(1,128)S(1)}) custom-call(f32[16,16384]{1,0:T(8,128)} %rate_hbm.1, f32[4,16,16384]{2,1,0:T(8,128)} %fx_hbm.1, f32[4]{0:T(128)} %vol_hbm.1, f32[4]{0:T(128)} %corr_hbm.1, f32[32]{0:T(128)} %scale_hbm.1, s32[1,512]{1,0:T(1,128)} %bitcast.6, s32[1,512]{1,0:T(1,128)} %bitcast.7, s32[1,512]{1,0:T(1,128)} %bitcast.8, ...), custom_call_target="tpu_custom_call" | custom-call | tf_op jit(solution)/shard_map/pallas_call | solution.py:511
  38.7 0.6 %shard_map.114 = (f32[16,32]{1,0:T(8,128)}, f32[1,32]{1,0:T(1,128)}) custom-call(f32[16,32]{1,0:T(8,128)S(1)} %get-tuple-element.6.profile, f32[1,32]{1,0:T(1,128)S(1)} %get-tuple-element.7.cva), custom_call_target="tpu_custom_call" | custom-call | tf_op jit(solution)/shard_map/pallas_call | solution.py:566
